TPU v7x, 32 devices: a 4x4x1 block of a 4x4x8 slice. The times are simulated.
32 devices in a mesh: dp: 1 (over z), sp: 32 (over y, x, core).
Axes of the slice: x: 4, y: 4, z: 1, core: 2. Of those that a mesh axis runs over, the one named last changes fastest.
The devices are a block of a 4x4x8 slice.
Arguments:
- x: bfloat16 [4, 2048, 512], P('dp', 'sp')
- w_in: bfloat16 [11, 3, 512, 1024], replicated
- w_res: bfloat16 [11, 512, 512], replicated
- w_skip: bfloat16 [11, 512, 512], replicated
Outputs:
- output 1: float32 [4, 2048, 512], P('dp', 'sp')
- output 2: float32 [4, 2048, 512], P('dp', 'sp')
All inputs are finite; a program needn't handle non-finite values.
Results may differ from a plain program's by a relative error of at most 0.00582507.
Values are sent between devices in bfloat16 or wider.
A program may use at most 768 MiB of HBM per device.

v0:
```python
import jax
import jax.numpy as jnp
from jax import lax
from jax.sharding import PartitionSpec as P


def neighbour_taps(cur_bf, dilation, n_dev):
    n_rows = cur_bf.shape[1]
    if dilation < n_rows:
        from_prev = lax.ppermute(cur_bf[:, n_rows - dilation:], 'sp', [(src, src + 1) for src in range(n_dev - 1)])
        from_next = lax.ppermute(cur_bf[:, :dilation], 'sp', [(src + 1, src) for src in range(n_dev - 1)])
        left_tap = jnp.concatenate([from_prev, cur_bf[:, :n_rows - dilation]], axis=1)
        right_tap = jnp.concatenate([cur_bf[:, dilation:], from_next], axis=1)
    else:
        n_hops = dilation // n_rows
        left_tap = lax.ppermute(cur_bf, 'sp', [(src, src + n_hops) for src in range(n_dev - n_hops)])
        right_tap = lax.ppermute(cur_bf, 'sp', [(src + n_hops, src) for src in range(n_dev - n_hops)])
    return left_tap, right_tap


def solution(mesh):
    n_dev = mesh.shape['sp']
    act_spec = P('dp', 'sp', None)

    def local_stack(x_local, w_in, w_res, w_skip):
        n_chan = x_local.shape[2]
        residual = x_local.astype(jnp.float32)
        skip_sum = jnp.zeros(x_local.shape[:2] + (w_skip.shape[2],), jnp.float32)
        for layer in range(w_in.shape[0]):
            cur_bf = residual.astype(jnp.bfloat16)
            left_tap, right_tap = neighbour_taps(cur_bf, 2 ** layer, n_dev)
            pre_act = (jnp.einsum('bsc,cf->bsf', left_tap, w_in[layer, 0], preferred_element_type=jnp.float32)
                       + jnp.einsum('bsc,cf->bsf', cur_bf, w_in[layer, 1], preferred_element_type=jnp.float32)
                       + jnp.einsum('bsc,cf->bsf', right_tap, w_in[layer, 2], preferred_element_type=jnp.float32))
            gated = (jnp.tanh(pre_act[..., :n_chan]) * jax.nn.sigmoid(pre_act[..., n_chan:])).astype(jnp.bfloat16)
            residual = residual + jnp.einsum('bsc,cf->bsf', gated, w_res[layer], preferred_element_type=jnp.float32)
            skip_sum = skip_sum + jnp.einsum('bsc,cf->bsf', gated, w_skip[layer], preferred_element_type=jnp.float32)
        return residual, skip_sum

    return jax.shard_map(local_stack, mesh=mesh, in_specs=(act_spec, P(), P(), P()), out_specs=(act_spec, act_spec), check_vma=False)
```

profile of v0, /device:TPU:120, one launch (start us, length us, event | category | flops | bytes accessed | tf_op | source)
XLA Modules:
  0.0 164.7 jit_solution(15008861367759892348)
XLA Ops:
  1.6 4.6 %collective-permute-start.1 = (bf16[4,1,512]{2,1,0:T(2,128)(2,1)S(1)}, bf16[4,1,512]{2,1,0:T(2,128)(2,1)S(1)}, u32[]{:S(2)}, u32[]{:S(2)}) collective-permute-start(bf16[4,1,512]{2,1,0:T(2,128)(2,1)S(1)} %get-tuple-element.21), channel_id=1, source_target_pairs={{1,0},{2,1},{3,2},{4,3},{5,4},{6,5},{7,6},{8,7},{9,8},{10,9},{11,1... | collective-permute-start | bytes 12296 | tf_op jit(solution)/shard_map/ppermute | solution.py:11
  6.3 2.3 %collective-permute-start = (bf16[4,1,512]{2,1,0:T(2,128)(2,1)S(1)}, bf16[4,1,512]{2,1,0:T(2,128)(2,1)S(1)}, u32[]{:S(2)}, u32[]{:S(2)}) collective-permute-start(bf16[4,1,512]{2,1,0:T(2,128)(2,1)S(1)} %get-tuple-element.20), channel_id=1, source_target_pairs={{0,1},{1,2},{2,3},{3,4},{4,5},{5,6},{6,7},{7,8},{8,9},{9,10},{10,1... | collective-permute-start | bytes 12296 | tf_op jit(solution)/shard_map/ppermute | solution.py:10
  8.6 2.6 %fusion.63 = f32[4,64,1024]{2,1,0:T(8,128)S(1)} fusion(bf16[4,64,512]{2,1,0:T(8,128)(2,1)} %param.4, bf16[11,3,512,1024]{3,2,1,0:T(8,128)(2,1)} %param.5), kind=kOutput, calls=%fused_computation.95 | convolution fusion | flops 268435456 | bytes 2359296 | tf_op jit(solution)/shard_map/bsc,cf->bsf/dot_general | solution.py:33
  11.2 2.0 %fusion.257 = (bf16[4,63,512]{2,1,0:T(8,128)(2,1)S(1)}, bf16[4,63,512]{2,1,0:T(8,128)(2,1)S(1)}) fusion(bf16[4,64,512]{2,1,0:T(8,128)(2,1)} %param.4), kind=kLoop, calls=%fused_computation.311 | loop fusion | bytes 1032192 | tf_op jit(solution)/shard_map/slice | solution.py:12
  13.2 2.4 %fusion.61 = f32[4,64,1024]{2,1,0:T(8,128)S(1)} fusion(bf16[11,3,512,1024]{3,2,1,0:T(8,128)(2,1)} %param.5, bf16[4,1,512]{2,1,0:T(2,128)(2,1)S(1)} %collective-permute-done.1, bf16[4,63,512]{2,1,0:T(8,128)(2,1)S(1)} %get-tuple-element.23), kind=kOutput, calls=%fused_computation.93 | convolution fusion | flops 268959744 | bytes 2359296 | tf_op jit(solution)/shard_map/bsc,cf->bsf/dot_general | solution.py:34
  20.6 5.0 %collective-permute-start.3 = (bf16[4,2,512]{2,1,0:T(2,128)(2,1)S(1)}, bf16[4,2,512]{2,1,0:T(2,128)(2,1)S(1)}, u32[]{:S(2)}, u32[]{:S(2)}) collective-permute-start(bf16[4,2,512]{2,1,0:T(2,128)(2,1)S(1)} %get-tuple-element.17), channel_id=1, source_target_pairs={{1,0},{2,1},{3,2},{4,3},{5,4},{6,5},{7,6},{8,7},{9,8},{10,9},{11,1... | collective-permute-start | bytes 24584 | tf_op jit(solution)/shard_map/ppermute | solution.py:11
  30.6 2.1 %collective-permute-done.2 = bf16[4,2,512]{2,1,0:T(2,128)(2,1)S(1)} collective-permute-done((bf16[4,2,512]{2,1,0:T(2,128)(2,1)S(1)}, bf16[4,2,512]{2,1,0:T(2,128)(2,1)S(1)}, u32[]{:S(2)}, u32[]{:S(2)}) %collective-permute-start.2) | collective-permute-done | bytes 8224 | tf_op jit(solution)/shard_map/ppermute | solution.py:10
  37.7 3.8 %collective-permute-start.5 = (bf16[4,4,512]{2,1,0:T(4,128)(2,1)S(1)}, bf16[4,4,512]{2,1,0:T(4,128)(2,1)S(1)}, u32[]{:S(2)}, u32[]{:S(2)}) collective-permute-start(bf16[4,4,512]{2,1,0:T(4,128)(2,1)S(1)} %get-tuple-element.13), channel_id=1, source_target_pairs={{1,0},{2,1},{3,2},{4,3},{5,4},{6,5},{7,6},{8,7},{9,8},{10,9},{11,1... | collective-permute-start | bytes 49160 | tf_op jit(solution)/shard_map/ppermute | solution.py:11
  46.6 2.1 %collective-permute-done.4 = bf16[4,4,512]{2,1,0:T(4,128)(2,1)S(1)} collective-permute-done((bf16[4,4,512]{2,1,0:T(4,128)(2,1)S(1)}, bf16[4,4,512]{2,1,0:T(4,128)(2,1)S(1)}, u32[]{:S(2)}, u32[]{:S(2)}) %collective-permute-start.4) | collective-permute-done | bytes 16416 | tf_op jit(solution)/shard_map/ppermute | solution.py:10
  50.5 3.7 %collective-permute-start.7 = (bf16[4,8,512]{2,1,0:T(8,128)(2,1)S(1)}, bf16[4,8,512]{2,1,0:T(8,128)(2,1)S(1)}, u32[]{:S(2)}, u32[]{:S(2)}) collective-permute-start(bf16[4,8,512]{2,1,0:T(8,128)(2,1)S(1)} %get-tuple-element.9), channel_id=1, source_target_pairs={{1,0},{2,1},{3,2},{4,3},{5,4},{6,5},{7,6},{8,7},{9,8},{10,9},{11,1... | collective-permute-start | bytes 98312 | tf_op jit(solution)/shard_map/ppermute | solution.py:11
  56.6 5.0 %collective-permute-done.6 = bf16[4,8,512]{2,1,0:T(8,128)(2,1)S(1)} collective-permute-done((bf16[4,8,512]{2,1,0:T(8,128)(2,1)S(1)}, bf16[4,8,512]{2,1,0:T(8,128)(2,1)S(1)}, u32[]{:S(2)}, u32[]{:S(2)}) %collective-permute-start.6) | collective-permute-done | bytes 32800 | tf_op jit(solution)/shard_map/ppermute | solution.py:10
  65.3 2.4 %collective-permute-start.8 = (bf16[4,16,512]{2,1,0:T(8,128)(2,1)S(1)}, bf16[4,16,512]{2,1,0:T(8,128)(2,1)S(1)}, u32[]{:S(2)}, u32[]{:S(2)}) collective-permute-start(bf16[4,16,512]{2,1,0:T(8,128)(2,1)S(1)} %get-tuple-element.4), channel_id=1, source_target_pairs={{0,1},{1,2},{2,3},{3,4},{4,5},{5,6},{6,7},{7,8},{8,9},{9,10},{10,1... | collective-permute-start | bytes 196616 | tf_op jit(solution)/shard_map/ppermute | solution.py:10
  68.2 4.8 %collective-permute-done.8 = bf16[4,16,512]{2,1,0:T(8,128)(2,1)S(1)} collective-permute-done((bf16[4,16,512]{2,1,0:T(8,128)(2,1)S(1)}, bf16[4,16,512]{2,1,0:T(8,128)(2,1)S(1)}, u32[]{:S(2)}, u32[]{:S(2)}) %collective-permute-start.8) | collective-permute-done | bytes 65568 | tf_op jit(solution)/shard_map/ppermute | solution.py:10
  76.8 2.4 %collective-permute-start.10 = (bf16[4,32,512]{2,1,0:T(8,128)(2,1)S(1)}, bf16[4,32,512]{2,1,0:T(8,128)(2,1)S(1)}, u32[]{:S(2)}, u32[]{:S(2)}) collective-permute-start(bf16[4,32,512]{2,1,0:T(8,128)(2,1)S(1)} %get-tuple-element.2), channel_id=1, source_target_pairs={{0,1},{1,2},{2,3},{3,4},{4,5},{5,6},{6,7},{7,8},{8,9},{9,10},{10,1... | collective-permute-start | bytes 393224 | tf_op jit(solution)/shard_map/ppermute | solution.py:10
  79.7 5.5 %collective-permute-done.10 = bf16[4,32,512]{2,1,0:T(8,128)(2,1)S(1)} collective-permute-done((bf16[4,32,512]{2,1,0:T(8,128)(2,1)S(1)}, bf16[4,32,512]{2,1,0:T(8,128)(2,1)S(1)}, u32[]{:S(2)}, u32[]{:S(2)}) %collective-permute-start.10) | collective-permute-done | bytes 131104 | tf_op jit(solution)/shard_map/ppermute | solution.py:10
  88.6 2.6 %collective-permute-start.12 = (bf16[4,64,512]{2,1,0:T(8,128)(2,1)S(1)}, bf16[4,64,512]{2,1,0:T(8,128)(2,1)S(1)}, u32[]{:S(2)}, u32[]{:S(2)}) collective-permute-start(bf16[4,64,512]{2,1,0:T(8,128)(2,1)S(1)} %get-tuple-element.34), channel_id=1, source_target_pairs={{0,1},{1,2},{2,3},{3,4},{4,5},{5,6},{6,7},{7,8},{8,9},{9,10},{10,1... | collective-permute-start | bytes 786440 | tf_op jit(solution)/shard_map/ppermute | solution.py:16
  92.4 6.0 %collective-permute-done.12 = bf16[4,64,512]{2,1,0:T(8,128)(2,1)S(1)} collective-permute-done((bf16[4,64,512]{2,1,0:T(8,128)(2,1)S(1)}, bf16[4,64,512]{2,1,0:T(8,128)(2,1)S(1)}, u32[]{:S(2)}, u32[]{:S(2)}) %collective-permute-start.12) | collective-permute-done | bytes 262176 | tf_op jit(solution)/shard_map/ppermute | solution.py:16
  101.8 4.0 %collective-permute-start.14 = (bf16[4,64,512]{2,1,0:T(8,128)(2,1)S(1)}, bf16[4,64,512]{2,1,0:T(8,128)(2,1)S(1)}, u32[]{:S(2)}, u32[]{:S(2)}) collective-permute-start(bf16[4,64,512]{2,1,0:T(8,128)(2,1)S(1)} %get-tuple-element.36), channel_id=1, source_target_pairs={{0,2},{1,3},{2,4},{3,5},{4,6},{5,7},{6,8},{7,9},{8,10},{9,11},{10,... | collective-permute-start | bytes 786440 | tf_op jit(solution)/shard_map/ppermute | solution.py:16
  108.1 5.6 %collective-permute-done.14 = bf16[4,64,512]{2,1,0:T(8,128)(2,1)S(1)} collective-permute-done((bf16[4,64,512]{2,1,0:T(8,128)(2,1)S(1)}, bf16[4,64,512]{2,1,0:T(8,128)(2,1)S(1)}, u32[]{:S(2)}, u32[]{:S(2)}) %collective-permute-start.14) | collective-permute-done | bytes 262176 | tf_op jit(solution)/shard_map/ppermute | solution.py:16
  117.1 5.5 %collective-permute-start.16 = (bf16[4,64,512]{2,1,0:T(8,128)(2,1)S(1)}, bf16[4,64,512]{2,1,0:T(8,128)(2,1)S(1)}, u32[]{:S(2)}, u32[]{:S(2)}) collective-permute-start(bf16[4,64,512]{2,1,0:T(8,128)(2,1)S(1)} %get-tuple-element.38), channel_id=1, source_target_pairs={{0,4},{1,5},{2,6},{3,7},{4,8},{5,9},{6,10},{7,11},{8,12},{9,13},{1... | collective-permute-start | bytes 786440 | tf_op jit(solution)/shard_map/ppermute | solution.py:16
  124.9 5.0 %collective-permute-done.16 = bf16[4,64,512]{2,1,0:T(8,128)(2,1)S(1)} collective-permute-done((bf16[4,64,512]{2,1,0:T(8,128)(2,1)S(1)}, bf16[4,64,512]{2,1,0:T(8,128)(2,1)S(1)}, u32[]{:S(2)}, u32[]{:S(2)}) %collective-permute-start.16) | collective-permute-done | bytes 262176 | tf_op jit(solution)/shard_map/ppermute | solution.py:16
  131.7 7.7 %collective-permute-start.19 = (bf16[4,64,512]{2,1,0:T(8,128)(2,1)S(1)}, bf16[4,64,512]{2,1,0:T(8,128)(2,1)S(1)}, u32[]{:S(2)}, u32[]{:S(2)}) collective-permute-start(bf16[4,64,512]{2,1,0:T(8,128)(2,1)S(1)} %get-tuple-element.40), channel_id=1, source_target_pairs={{8,0},{9,1},{10,2},{11,3},{12,4},{13,5},{14,6},{15,7},{16,8},{17,9... | collective-permute-start | bytes 786440 | tf_op jit(solution)/shard_map/ppermute | solution.py:17
  143.6 4.5 %collective-permute-done.18 = bf16[4,64,512]{2,1,0:T(8,128)(2,1)S(1)} collective-permute-done((bf16[4,64,512]{2,1,0:T(8,128)(2,1)S(1)}, bf16[4,64,512]{2,1,0:T(8,128)(2,1)S(1)}, u32[]{:S(2)}, u32[]{:S(2)}) %collective-permute-start.18) | collective-permute-done | bytes 262176 | tf_op jit(solution)/shard_map/ppermute | solution.py:16
  155.9 6.0 %collective-permute-done.20 = bf16[4,64,512]{2,1,0:T(8,128)(2,1)S(1)} collective-permute-done((bf16[4,64,512]{2,1,0:T(8,128)(2,1)S(1)}, bf16[4,64,512]{2,1,0:T(8,128)(2,1)S(1)}, u32[]{:S(2)}, u32[]{:S(2)}) %collective-permute-start.20) | collective-permute-done | bytes 262176 | tf_op jit(solution)/shard_map/ppermute | solution.py:16
  (106 shorter events, 65.9 us)
Async XLA Ops:
  0.6 48.7 %copy-start.1 = (bf16[11,512,512]{2,1,0:T(8,128)(2,1)S(1)}, bf16[11,512,512]{2,1,0:T(8,128)(2,1)}, u32[]{:S(2)}) copy-start(bf16[11,512,512]{2,1,0:T(8,128)(2,1)} %param.6) | copy-start | bytes 17301508
  0.7 49.5 %slice-start = ((s8[5767168]{0:T(1024)(128)(4,1)}), s8[4194304]{0:T(1024)(128)(4,1)S(1)}, s32[]{:S(2)}) async-start(s8[5767168]{0:T(1024)(128)(4,1)} %bitcast.316), calls=%async_computation | async-start | bytes 8388608
  1.6 11.6 %collective-permute-start.1 = (bf16[4,1,512]{2,1,0:T(2,128)(2,1)S(1)}, bf16[4,1,512]{2,1,0:T(2,128)(2,1)S(1)}, u32[]{:S(2)}, u32[]{:S(2)}) collective-permute-start(bf16[4,1,512]{2,1,0:T(2,128)(2,1)S(1)} %get-tuple-element.21), channel_id=1, source_target_pairs={{1,0},{2,1},{3,2},{4,3},{5,4},{6,5},{7,6},{8,7},{9,8},{10,9},{11,1... | collective-permute-start | bytes 12296 | tf_op jit(solution)/shard_map/ppermute | solution.py:11
  6.3 9.3 %collective-permute-start = (bf16[4,1,512]{2,1,0:T(2,128)(2,1)S(1)}, bf16[4,1,512]{2,1,0:T(2,128)(2,1)S(1)}, u32[]{:S(2)}, u32[]{:S(2)}) collective-permute-start(bf16[4,1,512]{2,1,0:T(2,128)(2,1)S(1)} %get-tuple-element.20), channel_id=1, source_target_pairs={{0,1},{1,2},{2,3},{3,4},{4,5},{5,6},{6,7},{7,8},{8,9},{9,10},{10,1... | collective-permute-start | bytes 12296 | tf_op jit(solution)/shard_map/ppermute | solution.py:10
  20.6 8.4 %collective-permute-start.3 = (bf16[4,2,512]{2,1,0:T(2,128)(2,1)S(1)}, bf16[4,2,512]{2,1,0:T(2,128)(2,1)S(1)}, u32[]{:S(2)}, u32[]{:S(2)}) collective-permute-start(bf16[4,2,512]{2,1,0:T(2,128)(2,1)S(1)} %get-tuple-element.17), channel_id=1, source_target_pairs={{1,0},{2,1},{3,2},{4,3},{5,4},{6,5},{7,6},{8,7},{9,8},{10,9},{11,1... | collective-permute-start | bytes 24584 | tf_op jit(solution)/shard_map/ppermute | solution.py:11
  25.6 7.1 %collective-permute-start.2 = (bf16[4,2,512]{2,1,0:T(2,128)(2,1)S(1)}, bf16[4,2,512]{2,1,0:T(2,128)(2,1)S(1)}, u32[]{:S(2)}, u32[]{:S(2)}) collective-permute-start(bf16[4,2,512]{2,1,0:T(2,128)(2,1)S(1)} %get-tuple-element.16), channel_id=1, source_target_pairs={{0,1},{1,2},{2,3},{3,4},{4,5},{5,6},{6,7},{7,8},{8,9},{9,10},{10,1... | collective-permute-start | bytes 24584 | tf_op jit(solution)/shard_map/ppermute | solution.py:10
  37.7 7.1 %collective-permute-start.5 = (bf16[4,4,512]{2,1,0:T(4,128)(2,1)S(1)}, bf16[4,4,512]{2,1,0:T(4,128)(2,1)S(1)}, u32[]{:S(2)}, u32[]{:S(2)}) collective-permute-start(bf16[4,4,512]{2,1,0:T(4,128)(2,1)S(1)} %get-tuple-element.13), channel_id=1, source_target_pairs={{1,0},{2,1},{3,2},{4,3},{5,4},{6,5},{7,6},{8,7},{9,8},{10,9},{11,1... | collective-permute-start | bytes 49160 | tf_op jit(solution)/shard_map/ppermute | solution.py:11
  41.5 7.2 %collective-permute-start.4 = (bf16[4,4,512]{2,1,0:T(4,128)(2,1)S(1)}, bf16[4,4,512]{2,1,0:T(4,128)(2,1)S(1)}, u32[]{:S(2)}, u32[]{:S(2)}) collective-permute-start(bf16[4,4,512]{2,1,0:T(4,128)(2,1)S(1)} %get-tuple-element.12), channel_id=1, source_target_pairs={{0,1},{1,2},{2,3},{3,4},{4,5},{5,6},{6,7},{7,8},{8,9},{9,10},{10,1... | collective-permute-start | bytes 49160 | tf_op jit(solution)/shard_map/ppermute | solution.py:10
  50.5 5.7 %collective-permute-start.7 = (bf16[4,8,512]{2,1,0:T(8,128)(2,1)S(1)}, bf16[4,8,512]{2,1,0:T(8,128)(2,1)S(1)}, u32[]{:S(2)}, u32[]{:S(2)}) collective-permute-start(bf16[4,8,512]{2,1,0:T(8,128)(2,1)S(1)} %get-tuple-element.9), channel_id=1, source_target_pairs={{1,0},{2,1},{3,2},{4,3},{5,4},{6,5},{7,6},{8,7},{9,8},{10,9},{11,1... | collective-permute-start | bytes 98312 | tf_op jit(solution)/shard_map/ppermute | solution.py:11
  54.2 7.4 %collective-permute-start.6 = (bf16[4,8,512]{2,1,0:T(8,128)(2,1)S(1)}, bf16[4,8,512]{2,1,0:T(8,128)(2,1)S(1)}, u32[]{:S(2)}, u32[]{:S(2)}) collective-permute-start(bf16[4,8,512]{2,1,0:T(8,128)(2,1)S(1)} %get-tuple-element.8), channel_id=1, source_target_pairs={{0,1},{1,2},{2,3},{3,4},{4,5},{5,6},{6,7},{7,8},{8,9},{9,10},{10,1... | collective-permute-start | bytes 98312 | tf_op jit(solution)/shard_map/ppermute | solution.py:10
  63.3 4.4 %collective-permute-start.9 = (bf16[4,16,512]{2,1,0:T(8,128)(2,1)S(1)}, bf16[4,16,512]{2,1,0:T(8,128)(2,1)S(1)}, u32[]{:S(2)}, u32[]{:S(2)}) collective-permute-start(bf16[4,16,512]{2,1,0:T(8,128)(2,1)S(1)} %get-tuple-element.5), channel_id=1, source_target_pairs={{1,0},{2,1},{3,2},{4,3},{5,4},{6,5},{7,6},{8,7},{9,8},{10,9},{11,1... | collective-permute-start | bytes 196616 | tf_op jit(solution)/shard_map/ppermute | solution.py:11
  65.3 7.7 %collective-permute-start.8 = (bf16[4,16,512]{2,1,0:T(8,128)(2,1)S(1)}, bf16[4,16,512]{2,1,0:T(8,128)(2,1)S(1)}, u32[]{:S(2)}, u32[]{:S(2)}) collective-permute-start(bf16[4,16,512]{2,1,0:T(8,128)(2,1)S(1)} %get-tuple-element.4), channel_id=1, source_target_pairs={{0,1},{1,2},{2,3},{3,4},{4,5},{5,6},{6,7},{7,8},{8,9},{9,10},{10,1... | collective-permute-start | bytes 196616 | tf_op jit(solution)/shard_map/ppermute | solution.py:10
  74.5 4.7 %collective-permute-start.11 = (bf16[4,32,512]{2,1,0:T(8,128)(2,1)S(1)}, bf16[4,32,512]{2,1,0:T(8,128)(2,1)S(1)}, u32[]{:S(2)}, u32[]{:S(2)}) collective-permute-start(bf16[4,32,512]{2,1,0:T(8,128)(2,1)S(1)} %get-tuple-element.3), channel_id=1, source_target_pairs={{1,0},{2,1},{3,2},{4,3},{5,4},{6,5},{7,6},{8,7},{9,8},{10,9},{11,1... | collective-permute-start | bytes 393224 | tf_op jit(solution)/shard_map/ppermute | solution.py:11
  76.8 8.4 %collective-permute-start.10 = (bf16[4,32,512]{2,1,0:T(8,128)(2,1)S(1)}, bf16[4,32,512]{2,1,0:T(8,128)(2,1)S(1)}, u32[]{:S(2)}, u32[]{:S(2)}) collective-permute-start(bf16[4,32,512]{2,1,0:T(8,128)(2,1)S(1)} %get-tuple-element.2), channel_id=1, source_target_pairs={{0,1},{1,2},{2,3},{3,4},{4,5},{5,6},{6,7},{7,8},{8,9},{9,10},{10,1... | collective-permute-start | bytes 393224 | tf_op jit(solution)/shard_map/ppermute | solution.py:10
  86.2 5.8 %collective-permute-start.13 = (bf16[4,64,512]{2,1,0:T(8,128)(2,1)S(1)}, bf16[4,64,512]{2,1,0:T(8,128)(2,1)S(1)}, u32[]{:S(2)}, u32[]{:S(2)}) collective-permute-start(bf16[4,64,512]{2,1,0:T(8,128)(2,1)S(1)} %get-tuple-element.34), channel_id=1, source_target_pairs={{1,0},{2,1},{3,2},{4,3},{5,4},{6,5},{7,6},{8,7},{9,8},{10,9},{11,1... | collective-permute-start | bytes 786440 | tf_op jit(solution)/shard_map/ppermute | solution.py:17
  88.6 9.8 %collective-permute-start.12 = (bf16[4,64,512]{2,1,0:T(8,128)(2,1)S(1)}, bf16[4,64,512]{2,1,0:T(8,128)(2,1)S(1)}, u32[]{:S(2)}, u32[]{:S(2)}) collective-permute-start(bf16[4,64,512]{2,1,0:T(8,128)(2,1)S(1)} %get-tuple-element.34), channel_id=1, source_target_pairs={{0,1},{1,2},{2,3},{3,4},{4,5},{5,6},{6,7},{7,8},{8,9},{9,10},{10,1... | collective-permute-start | bytes 786440 | tf_op jit(solution)/shard_map/ppermute | solution.py:16
  99.4 8.3 %collective-permute-start.15 = (bf16[4,64,512]{2,1,0:T(8,128)(2,1)S(1)}, bf16[4,64,512]{2,1,0:T(8,128)(2,1)S(1)}, u32[]{:S(2)}, u32[]{:S(2)}) collective-permute-start(bf16[4,64,512]{2,1,0:T(8,128)(2,1)S(1)} %get-tuple-element.36), channel_id=1, source_target_pairs={{2,0},{3,1},{4,2},{5,3},{6,4},{7,5},{8,6},{9,7},{10,8},{11,9},{12,... | collective-permute-start | bytes 786440 | tf_op jit(solution)/shard_map/ppermute | solution.py:17
  101.8 11.9 %collective-permute-start.14 = (bf16[4,64,512]{2,1,0:T(8,128)(2,1)S(1)}, bf16[4,64,512]{2,1,0:T(8,128)(2,1)S(1)}, u32[]{:S(2)}, u32[]{:S(2)}) collective-permute-start(bf16[4,64,512]{2,1,0:T(8,128)(2,1)S(1)} %get-tuple-element.36), channel_id=1, source_target_pairs={{0,2},{1,3},{2,4},{3,5},{4,6},{5,7},{6,8},{7,9},{8,10},{9,11},{10,... | collective-permute-start | bytes 786440 | tf_op jit(solution)/shard_map/ppermute | solution.py:16
  114.7 9.8 %collective-permute-start.17 = (bf16[4,64,512]{2,1,0:T(8,128)(2,1)S(1)}, bf16[4,64,512]{2,1,0:T(8,128)(2,1)S(1)}, u32[]{:S(2)}, u32[]{:S(2)}) collective-permute-start(bf16[4,64,512]{2,1,0:T(8,128)(2,1)S(1)} %get-tuple-element.38), channel_id=1, source_target_pairs={{4,0},{5,1},{6,2},{7,3},{8,4},{9,5},{10,6},{11,7},{12,8},{13,9},{1... | collective-permute-start | bytes 786440 | tf_op jit(solution)/shard_map/ppermute | solution.py:17
  117.1 12.9 %collective-permute-start.16 = (bf16[4,64,512]{2,1,0:T(8,128)(2,1)S(1)}, bf16[4,64,512]{2,1,0:T(8,128)(2,1)S(1)}, u32[]{:S(2)}, u32[]{:S(2)}) collective-permute-start(bf16[4,64,512]{2,1,0:T(8,128)(2,1)S(1)} %get-tuple-element.38), channel_id=1, source_target_pairs={{0,4},{1,5},{2,6},{3,7},{4,8},{5,9},{6,10},{7,11},{8,12},{9,13},{1... | collective-permute-start | bytes 786440 | tf_op jit(solution)/shard_map/ppermute | solution.py:16
  131.7 11.5 %collective-permute-start.19 = (bf16[4,64,512]{2,1,0:T(8,128)(2,1)S(1)}, bf16[4,64,512]{2,1,0:T(8,128)(2,1)S(1)}, u32[]{:S(2)}, u32[]{:S(2)}) collective-permute-start(bf16[4,64,512]{2,1,0:T(8,128)(2,1)S(1)} %get-tuple-element.40), channel_id=1, source_target_pairs={{8,0},{9,1},{10,2},{11,3},{12,4},{13,5},{14,6},{15,7},{16,8},{17,9... | collective-permute-start | bytes 786440 | tf_op jit(solution)/shard_map/ppermute | solution.py:17
  139.8 8.3 %collective-permute-start.18 = (bf16[4,64,512]{2,1,0:T(8,128)(2,1)S(1)}, bf16[4,64,512]{2,1,0:T(8,128)(2,1)S(1)}, u32[]{:S(2)}, u32[]{:S(2)}) collective-permute-start(bf16[4,64,512]{2,1,0:T(8,128)(2,1)S(1)} %get-tuple-element.40), channel_id=1, source_target_pairs={{0,8},{1,9},{2,10},{3,11},{4,12},{5,13},{6,14},{7,15},{8,16},{9,17... | collective-permute-start | bytes 786440 | tf_op jit(solution)/shard_map/ppermute | solution.py:16
  150.1 5.4 %collective-permute-start.21 = (bf16[4,64,512]{2,1,0:T(8,128)(2,1)S(1)}, bf16[4,64,512]{2,1,0:T(8,128)(2,1)S(1)}, u32[]{:S(2)}, u32[]{:S(2)}) collective-permute-start(bf16[4,64,512]{2,1,0:T(8,128)(2,1)S(1)} %get-tuple-element.42), channel_id=1, source_target_pairs={{16,0},{17,1},{18,2},{19,3},{20,4},{21,5},{22,6},{23,7},{24,8},{25... | collective-permute-start | bytes 786440 | tf_op jit(solution)/shard_map/ppermute | solution.py:17
  152.1 9.8 %collective-permute-start.20 = (bf16[4,64,512]{2,1,0:T(8,128)(2,1)S(1)}, bf16[4,64,512]{2,1,0:T(8,128)(2,1)S(1)}, u32[]{:S(2)}, u32[]{:S(2)}) collective-permute-start(bf16[4,64,512]{2,1,0:T(8,128)(2,1)S(1)} %get-tuple-element.42), channel_id=1, source_target_pairs={{0,16},{1,17},{2,18},{3,19},{4,20},{5,21},{6,22},{7,23},{8,24},{9,... | collective-permute-start | bytes 786440 | tf_op jit(solution)/shard_map/ppermute | solution.py:16
  (2 other events, 65.6 us)
where the time goes:
time: 166 us; the launch traced here: 165 us
  starting transfers between devices  63.7 us (38%)
  waiting for transfers between devices  53.8 us (32%)
  matrix products  40.2 us (24%)
  local copies, waits for them, and re-layouts  3.2 us (2%)
  other arithmetic  2.35 us (1%)
    ppermute x5, waiting for transfers between devices, neighbour_taps(): lax.ppermute(cur_bf, 'sp', [(src, src + n_hops) for src in range(n_dev -...  27 us
    ppermute x6, starting transfers between devices, neighbour_taps(): lax.ppermute(cur_bf[:, :dilation], 'sp', [(src + 1, src) for src in range...  20.9 us
    ppermute x6, waiting for transfers between devices, neighbour_taps(): lax.ppermute(cur_bf[:, n_rows - dilation:], 'sp', [(src, src + 1) for src...  19.5 us
    ppermute x5, starting transfers between devices, neighbour_taps(): lax.ppermute(cur_bf, 'sp', [(src + n_hops, src) for src in range(n_dev -...  15 us
    ppermute x5, starting transfers between devices, neighbour_taps(): lax.ppermute(cur_bf, 'sp', [(src, src + n_hops) for src in range(n_dev -...  14.7 us
    ppermute x6, starting transfers between devices, neighbour_taps(): lax.ppermute(cur_bf[:, n_rows - dilation:], 'sp', [(src, src + 1) for src...  13.1 us
    dot_general x11, matrix products, local_stack(): jnp.einsum('bsc,cf->bsf', cur_bf, w_in[layer, 1], preferred_element_type=...  9.39 us
    dot_general x11, matrix products, local_stack(): jnp.einsum('bsc,cf->bsf', right_tap, w_in[layer, 2], preferred_element_ty...  9.17 us
  transfers between devices with their start and end apart: 22, of which 15 were waited for; matrix products, arithmetic and copies ran while one was open for 12% of the time, Pallas kernels for 0%

commit v1 on v0

v1 whole, which is shorter than its diff:
```python
import functools

import jax
import jax.numpy as jnp
from jax import lax
from jax.experimental import pallas as pl
from jax.experimental.pallas import tpu as pltpu
from jax.sharding import PartitionSpec as P

MESH = pl.DeviceIdType.MESH
F32, BF16 = jnp.float32, jnp.bfloat16
TILE = 8
HALO = 8
EDGE = 16
COLS = 256


def stack_kernel(n_dev, n_near, x_hbm, win_hbm, wres_hbm, wskip_hbm, h_out, s_out, win, wres, wskip, xv, halo_l, halo_r,
                 near, near_skip, out_blocks, far, far_skip, home_h, home_s, lhs, gate,
                 x_sem, w_sem, halo_send, halo_recv, mid_send, mid_recv, end_send, end_recv):
    me = lax.axis_index('sp')
    n_seq, rows, n_chan = xv.shape
    n_skip = far_skip.shape[1]
    n_layers = win.shape[0]
    far_rows = far_skip.shape[0]
    pad = (far.shape[0] - far_rows) // 2
    n_res = rows // TILE
    last = n_dev - 1

    barrier = pltpu.get_barrier_semaphore()

    @pl.loop(1, n_dev)
    def _(k):
        pl.semaphore_signal(barrier, inc=1, device_id={'sp': lax.rem(me + k, n_dev)}, device_id_type=MESH)

    x_copy = pltpu.make_async_copy(x_hbm, xv, x_sem)
    x_copy.start()

    def weight_copies(layer):
        return [pltpu.make_async_copy(win_hbm.at[layer], win.at[layer], w_sem.at[layer, 0]),
                pltpu.make_async_copy(wres_hbm.at[layer], wres.at[layer], w_sem.at[layer, 1]),
                pltpu.make_async_copy(wskip_hbm.at[layer], wskip.at[layer], w_sem.at[layer, 2])]

    for layer in range(n_layers):
        for copy in weight_copies(layer):
            copy.start()

    zero_edge = jnp.zeros((n_seq, EDGE, n_chan), F32)
    near[:, :EDGE] = zero_edge
    near[:, EDGE + rows:] = zero_edge
    far[:pad] = jnp.zeros((pad, n_chan), F32)
    far[pad + far_rows:] = jnp.zeros((pad, n_chan), F32)

    x_copy.wait()
    pl.semaphore_wait(barrier, n_dev - 1)

    def to_next():
        return pltpu.make_async_remote_copy(src_ref=xv.at[:, pl.ds(rows - HALO, HALO)], dst_ref=halo_l, send_sem=halo_send.at[0],
                                            recv_sem=halo_recv.at[0], device_id={'sp': me + 1}, device_id_type=MESH)

    def to_prev():
        return pltpu.make_async_remote_copy(src_ref=xv.at[:, pl.ds(0, HALO)], dst_ref=halo_r, send_sem=halo_send.at[1],
                                            recv_sem=halo_recv.at[1], device_id={'sp': me - 1}, device_id_type=MESH)

    @pl.when(me < last)
    def _():
        to_next().start()

    @pl.when(me > 0)
    def _():
        to_prev().start()

    near[:, EDGE:EDGE + rows] = xv[...].astype(F32)

    @pl.when(me > 0)
    def _():
        to_next().wait_recv()
        near[:, EDGE - HALO:EDGE] = halo_l[...].astype(F32)

    @pl.when(me < last)
    def _():
        to_prev().wait_recv()
        near[:, EDGE + rows:EDGE + rows + HALO] = halo_r[...].astype(F32)

    def gated_layer(layer, m):
        w = win.at[layer]
        for col in range(0, n_chan, COLS):
            f = jnp.zeros((m, COLS), F32)
            g = jnp.zeros((m, COLS), F32)
            for tap in range(3):
                op = lhs[:m, tap * n_chan:(tap + 1) * n_chan]
                f = f + jnp.dot(op, w[tap, :, col:col + COLS], preferred_element_type=F32)
                g = g + jnp.dot(op, w[tap, :, n_chan + col:n_chan + col + COLS], preferred_element_type=F32)
            gate[:m, col:col + COLS] = (jnp.tanh(f) * (0.5 * jnp.tanh(0.5 * g) + 0.5)).astype(BF16)

    for layer in range(n_near):
        dist = 2 ** layer
        lo, hi = (EDGE - HALO, EDGE + rows + HALO) if layer < n_near - 1 else (EDGE, EDGE + rows)
        size = hi - lo
        m = n_seq * size
        for tap in range(3):
            off = lo + (tap - 1) * dist
            for seq in range(n_seq):
                lhs[seq * size:(seq + 1) * size, tap * n_chan:(tap + 1) * n_chan] = near[seq, off:off + size].astype(BF16)
        for copy in weight_copies(layer):
            copy.wait()
        gated_layer(layer, m)
        for col in range(0, n_chan, COLS):
            res = jnp.dot(gate[:m], wres[layer, :, col:col + COLS], preferred_element_type=F32).reshape(n_seq, size, COLS)
            near[:, lo:hi, col:col + COLS] = near[:, lo:hi, col:col + COLS] + res
        for col in range(0, n_skip, COLS):
            skip = jnp.dot(gate[:m], wskip[layer, :, col:col + COLS], preferred_element_type=F32).reshape(n_seq, size, COLS)
            skip = skip[:, EDGE - lo:EDGE - lo + rows]
            if layer:
                skip = near_skip[:, :, col:col + COLS] + skip
            near_skip[:, :, col:col + COLS] = skip
        if layer < n_near - 1:
            @pl.when(me == 0)
            def _():
                near[:, :EDGE] = zero_edge

            @pl.when(me == last)
            def _():
                near[:, EDGE + rows:] = zero_edge

    for seq in range(n_seq):
        own = near[seq, EDGE:EDGE + rows].reshape(TILE, n_res, n_chan)
        out_blocks[seq * n_res:(seq + 1) * n_res] = jnp.swapaxes(own, 0, 1)

    def mid_copy(dst, src):
        return pltpu.make_async_remote_copy(src_ref=out_blocks.at[dst], dst_ref=far.at[pl.ds(pl.multiple_of(pad + src * TILE, TILE), TILE)],
                                            send_sem=mid_send.at[dst], recv_sem=mid_recv.at[src], device_id={'sp': dst}, device_id_type=MESH)

    @pl.loop(1, n_dev)
    def _(k):
        mid_copy(lax.rem(me + k, n_dev), me).start()

    far[pl.ds(pl.multiple_of(pad + me * TILE, TILE), TILE)] = out_blocks[me]

    @pl.loop(1, n_dev)
    def _(k):
        src = lax.rem(me + n_dev - k, n_dev)
        mid_copy(lax.rem(me + k, n_dev), src).wait_recv()

    for layer in range(n_near, n_layers):
        dist = 2 ** layer // n_res
        for tap in range(3):
            off = pad + (tap - 1) * dist
            lhs[:far_rows, tap * n_chan:(tap + 1) * n_chan] = far[off:off + far_rows].astype(BF16)
        for copy in weight_copies(layer):
            copy.wait()
        gated_layer(layer, far_rows)
        for col in range(0, n_chan, COLS):
            res = jnp.dot(gate[:far_rows], wres[layer, :, col:col + COLS], preferred_element_type=F32)
            far[pad:pad + far_rows, col:col + COLS] = far[pad:pad + far_rows, col:col + COLS] + res
        for col in range(0, n_skip, COLS):
            skip = jnp.dot(gate[:far_rows], wskip[layer, :, col:col + COLS], preferred_element_type=F32)
            if layer > n_near:
                skip = far_skip[:, col:col + COLS] + skip
            far_skip[:, col:col + COLS] = skip

    def end_copy(which, dst, src):
        source = far.at[pl.ds(pl.multiple_of(pad + dst * TILE, TILE), TILE)] if which == 0 else far_skip.at[pl.ds(pl.multiple_of(dst * TILE, TILE), TILE)]
        return pltpu.make_async_remote_copy(src_ref=source, dst_ref=(home_h, home_s)[which].at[src],
                                            send_sem=end_send.at[which, dst], recv_sem=end_recv.at[which, src], device_id={'sp': dst}, device_id_type=MESH)

    for which in range(2):
        @pl.loop(1, n_dev)
        def _(k):
            end_copy(which, lax.rem(me + k, n_dev), me).start()

    home_h[me] = far[pl.ds(pl.multiple_of(pad + me * TILE, TILE), TILE)]
    home_s[me] = far_skip[pl.ds(pl.multiple_of(me * TILE, TILE), TILE)]

    for which in range(2):
        @pl.loop(1, n_dev)
        def _(k):
            end_copy(which, lax.rem(me + k, n_dev), lax.rem(me + n_dev - k, n_dev)).wait_recv()

    for seq in range(n_seq):
        blocks = slice(seq * n_res, (seq + 1) * n_res)
        h_out[seq] = jnp.swapaxes(home_h[blocks], 0, 1).reshape(rows, n_chan)
        s_out[seq] = jnp.swapaxes(home_s[blocks], 0, 1).reshape(rows, n_skip) + near_skip[seq]

    @pl.when(me < last)
    def _():
        to_next().wait_send()

    @pl.when(me > 0)
    def _():
        to_prev().wait_send()

    @pl.loop(1, n_dev)
    def _(k):
        dst = lax.rem(me + k, n_dev)
        mid_copy(dst, me).wait_send()
        end_copy(0, dst, me).wait_send()
        end_copy(1, dst, me).wait_send()


def solution(mesh):
    n_dev = mesh.shape['sp']
    act_spec = P('dp', 'sp', None)

    def local_stack(x, w_in, w_res, w_skip):
        n_seq, rows, n_chan = x.shape
        n_layers, n_skip = w_in.shape[0], w_skip.shape[2]
        n_res = n_dev // n_seq
        n_near = n_res.bit_length() - 1
        far_rows = n_dev * rows // n_res
        pad = 2 ** (n_layers - 1) // n_res
        any_spec = pl.BlockSpec(memory_space=pl.ANY)
        vmem = pl.BlockSpec(memory_space=pltpu.VMEM)
        m_max = n_seq * (rows + 2 * HALO)
        dma = pltpu.SemaphoreType.DMA
        return pl.pallas_call(
            functools.partial(stack_kernel, n_dev, n_near),
            out_shape=(jax.ShapeDtypeStruct((n_seq, rows, n_chan), F32), jax.ShapeDtypeStruct((n_seq, rows, n_skip), F32)),
            in_specs=[any_spec] * 4,
            out_specs=(vmem, vmem),
            scratch_shapes=[
                pltpu.VMEM(w_in.shape, BF16), pltpu.VMEM(w_res.shape, BF16), pltpu.VMEM(w_skip.shape, BF16),
                pltpu.VMEM(x.shape, BF16), pltpu.VMEM((n_seq, HALO, n_chan), BF16), pltpu.VMEM((n_seq, HALO, n_chan), BF16),
                pltpu.VMEM((n_seq, rows + 2 * EDGE, n_chan), F32), pltpu.VMEM((n_seq, rows, n_skip), F32),
                pltpu.VMEM((n_dev, TILE, n_chan), F32),
                pltpu.VMEM((far_rows + 2 * pad, n_chan), F32), pltpu.VMEM((far_rows, n_skip), F32),
                pltpu.VMEM((n_dev, TILE, n_chan), F32), pltpu.VMEM((n_dev, TILE, n_skip), F32),
                pltpu.VMEM((m_max, 3 * n_chan), BF16), pltpu.VMEM((m_max, n_chan), BF16),
                dma, dma((n_layers, 3)), dma((2,)), dma((2,)), dma((n_dev,)), dma((n_dev,)), dma((2, n_dev)), dma((2, n_dev)),
            ],
            compiler_params=pltpu.CompilerParams(collective_id=0, has_side_effects=True, vmem_limit_bytes=63 * 2 ** 20),
            name='dilated_stack',
        )(x, w_in, w_res, w_skip)

    return jax.shard_map(local_stack, mesh=mesh, in_specs=(act_spec, P(), P(), P()), out_specs=(act_spec, act_spec), check_vma=False)
```

time: 166 us -> 69.4 us (0.42)
  the two profiles are of different devices: /device:TPU:120 before, /device:TPU:97 now
where the time goes in v1:
time: 69.4 us; the launch traced here: 69.2 us
  Pallas kernels  64.8 us (93%)
  local copies, waits for them, and re-layouts  3.74 us (5%)
    pallas_call x1, Pallas kernels, local_stack(): pl.pallas_call(functools.partial(stack_kernel, n_dev, n_near), out_shape=...  64.8 us
    unnamed x2, local copies, waits for them, and re-layouts  3.74 us

profile of v1, /device:TPU:97, one launch (start us, length us, event | category | flops | bytes accessed | tf_op | source)
XLA Modules:
  0.0 69.2 jit_solution(9978101440830663080)
XLA Ops:
  0.6 64.8 %dilated_stack.1 = (f32[4,64,512]{2,1,0:T(8,128)}, f32[4,64,512]{2,1,0:T(8,128)}) custom-call(bf16[4,64,512]{2,1,0:T(8,128)(2,1)} %x_hbm.1, bf16[11,3,512,1024]{3,2,1,0:T(8,128)(2,1)} %win_hbm.1, bf16[11,512,512]{2,1,0:T(8,128)(2,1)} %wres_hbm.1, bf16[11,512,512]{2,1,0:T(8,128)(2,1)} %wskip_hbm.1), custom_call_target="tpu_custom_call" | custom-call | tf_op jit(solution)/shard_map/dilated_stack/pallas_call | solution.py:216
  65.5 1.9 %copy.8 = f32[4,64,512]{2,1,0:T(8,128)} copy(f32[4,64,512]{2,1,0:T(8,128)} %get-tuple-element.4) | data formatting | bytes 1048576
  67.3 1.9 %copy.9 = f32[4,64,512]{2,1,0:T(8,128)} copy(f32[4,64,512]{2,1,0:T(8,128)} %get-tuple-element.5) | data formatting | bytes 1048576

commit v2 on v1

--- a/solution.py
+++ b/solution.py
@@ -15,9 +15,9 @@
 COLS = 256
 
 
-def stack_kernel(n_dev, n_near, x_hbm, win_hbm, wres_hbm, wskip_hbm, h_out, s_out, win, wres, wskip, xv, halo_l, halo_r,
-                 near, near_skip, out_blocks, far, far_skip, home_h, home_s, lhs, gate,
-                 x_sem, w_sem, halo_send, halo_recv, mid_send, mid_recv, end_send, end_recv):
+def stack_kernel(n_dev, n_near, x_hbm, win_hbm, wres_hbm, wskip_hbm, home_h, home_s, skip_out, win, wres, wskip, xv, halo_l, halo_r,
+                 near, near_skip, out_blocks, far, far_skip, lhs, gate, near_gate,
+                 x_sem, own_sem, w_sem, halo_send, halo_recv, mid_send, mid_recv, end_send, end_recv):
     me = lax.axis_index('sp')
     n_seq, rows, n_chan = xv.shape
     n_skip = far_skip.shape[1]
@@ -41,10 +41,6 @@
                 pltpu.make_async_copy(wres_hbm.at[layer], wres.at[layer], w_sem.at[layer, 1]),
                 pltpu.make_async_copy(wskip_hbm.at[layer], wskip.at[layer], w_sem.at[layer, 2])]
 
-    for layer in range(n_layers):
-        for copy in weight_copies(layer):
-            copy.start()
-
     zero_edge = jnp.zeros((n_seq, EDGE, n_chan), F32)
     near[:, :EDGE] = zero_edge
     near[:, EDGE + rows:] = zero_edge
@@ -52,6 +48,9 @@
     far[pad + far_rows:] = jnp.zeros((pad, n_chan), F32)
 
     x_copy.wait()
+    for layer in range(n_near):
+        for copy in weight_copies(layer):
+            copy.start()
     pl.semaphore_wait(barrier, n_dev - 1)
 
     def to_next():
@@ -104,16 +103,17 @@
                 lhs[seq * size:(seq + 1) * size, tap * n_chan:(tap + 1) * n_chan] = near[seq, off:off + size].astype(BF16)
         for copy in weight_copies(layer):
             copy.wait()
+        if layer == n_near - 1:
+            for later in range(n_near, n_layers):
+                for copy in weight_copies(later):
+                    copy.start()
         gated_layer(layer, m)
+        for seq in range(n_seq):
+            begin = seq * size + EDGE - lo
+            near_gate[seq * rows:(seq + 1) * rows, layer * n_chan:(layer + 1) * n_chan] = gate[begin:begin + rows]
         for col in range(0, n_chan, COLS):
             res = jnp.dot(gate[:m], wres[layer, :, col:col + COLS], preferred_element_type=F32).reshape(n_seq, size, COLS)
             near[:, lo:hi, col:col + COLS] = near[:, lo:hi, col:col + COLS] + res
-        for col in range(0, n_skip, COLS):
-            skip = jnp.dot(gate[:m], wskip[layer, :, col:col + COLS], preferred_element_type=F32).reshape(n_seq, size, COLS)
-            skip = skip[:, EDGE - lo:EDGE - lo + rows]
-            if layer:
-                skip = near_skip[:, :, col:col + COLS] + skip
-            near_skip[:, :, col:col + COLS] = skip
         if layer < n_near - 1:
             @pl.when(me == 0)
             def _():
@@ -137,10 +137,34 @@
 
     far[pl.ds(pl.multiple_of(pad + me * TILE, TILE), TILE)] = out_blocks[me]
 
+    for col in range(0, n_skip, COLS):
+        skip = jnp.zeros((n_seq * rows, COLS), F32)
+        for layer in range(n_near):
+            skip = skip + jnp.dot(near_gate[:, layer * n_chan:(layer + 1) * n_chan], wskip[layer, :, col:col + COLS], preferred_element_type=F32)
+        near_skip[:, :, col:col + COLS] = skip.reshape(n_seq, rows, COLS)
+    skip_copy = pltpu.make_async_copy(near_skip, skip_out, own_sem.at[2])
+    skip_copy.start()
+
     @pl.loop(1, n_dev)
     def _(k):
         src = lax.rem(me + n_dev - k, n_dev)
         mid_copy(lax.rem(me + k, n_dev), src).wait_recv()
+
+    def end_copy(which, dst, src):
+        source = far.at[pl.ds(pl.multiple_of(pad + dst * TILE, TILE), TILE)] if which == 0 else far_skip.at[pl.ds(pl.multiple_of(dst * TILE, TILE), TILE)]
+        return pltpu.make_async_remote_copy(src_ref=source, dst_ref=(home_h, home_s)[which].at[src],
+                                            send_sem=end_send.at[which, dst], recv_sem=end_recv.at[which, src], device_id={'sp': dst}, device_id_type=MESH)
+
+    def own_copy(which):
+        source = far.at[pl.ds(pl.multiple_of(pad + me * TILE, TILE), TILE)] if which == 0 else far_skip.at[pl.ds(pl.multiple_of(me * TILE, TILE), TILE)]
+        return pltpu.make_async_copy(source, (home_h, home_s)[which].at[me], own_sem.at[which])
+
+    def send_home(which):
+        @pl.loop(1, n_dev)
+        def _(k):
+            end_copy(which, lax.rem(me + k, n_dev), me).start()
+
+        own_copy(which).start()
 
     for layer in range(n_near, n_layers):
         dist = 2 ** layer // n_res
@@ -153,34 +177,24 @@
         for col in range(0, n_chan, COLS):
             res = jnp.dot(gate[:far_rows], wres[layer, :, col:col + COLS], preferred_element_type=F32)
             far[pad:pad + far_rows, col:col + COLS] = far[pad:pad + far_rows, col:col + COLS] + res
+        if layer == n_layers - 1:
+            send_home(0)
         for col in range(0, n_skip, COLS):
             skip = jnp.dot(gate[:far_rows], wskip[layer, :, col:col + COLS], preferred_element_type=F32)
             if layer > n_near:
                 skip = far_skip[:, col:col + COLS] + skip
             far_skip[:, col:col + COLS] = skip
 
-    def end_copy(which, dst, src):
-        source = far.at[pl.ds(pl.multiple_of(pad + dst * TILE, TILE), TILE)] if which == 0 else far_skip.at[pl.ds(pl.multiple_of(dst * TILE, TILE), TILE)]
-        return pltpu.make_async_remote_copy(src_ref=source, dst_ref=(home_h, home_s)[which].at[src],
-                                            send_sem=end_send.at[which, dst], recv_sem=end_recv.at[which, src], device_id={'sp': dst}, device_id_type=MESH)
-
-    for which in range(2):
-        @pl.loop(1, n_dev)
-        def _(k):
-            end_copy(which, lax.rem(me + k, n_dev), me).start()
-
-    home_h[me] = far[pl.ds(pl.multiple_of(pad + me * TILE, TILE), TILE)]
-    home_s[me] = far_skip[pl.ds(pl.multiple_of(me * TILE, TILE), TILE)]
+    send_home(1)
 
     for which in range(2):
         @pl.loop(1, n_dev)
         def _(k):
             end_copy(which, lax.rem(me + k, n_dev), lax.rem(me + n_dev - k, n_dev)).wait_recv()
 
-    for seq in range(n_seq):
-        blocks = slice(seq * n_res, (seq + 1) * n_res)
-        h_out[seq] = jnp.swapaxes(home_h[blocks], 0, 1).reshape(rows, n_chan)
-        s_out[seq] = jnp.swapaxes(home_s[blocks], 0, 1).reshape(rows, n_skip) + near_skip[seq]
+    skip_copy.wait()
+    own_copy(0).wait()
+    own_copy(1).wait()
 
     @pl.when(me < last)
     def _():
@@ -196,6 +210,12 @@
         mid_copy(dst, me).wait_send()
         end_copy(0, dst, me).wait_send()
         end_copy(1, dst, me).wait_send()
+
+
+def assemble_kernel(h_blocks, s_blocks, skip, h_out, s_out):
+    n_res = h_blocks.shape[0]
+    h_out[0] = jnp.swapaxes(h_blocks[...], 0, 1).reshape(h_out.shape[1:])
+    s_out[0] = jnp.swapaxes(s_blocks[...], 0, 1).reshape(s_out.shape[1:]) + skip[0]
 
 
 def solution(mesh):
@@ -210,26 +230,35 @@
         far_rows = n_dev * rows // n_res
         pad = 2 ** (n_layers - 1) // n_res
         any_spec = pl.BlockSpec(memory_space=pl.ANY)
-        vmem = pl.BlockSpec(memory_space=pltpu.VMEM)
         m_max = n_seq * (rows + 2 * HALO)
         dma = pltpu.SemaphoreType.DMA
-        return pl.pallas_call(
+        home_h, home_s, skip = pl.pallas_call(
             functools.partial(stack_kernel, n_dev, n_near),
-            out_shape=(jax.ShapeDtypeStruct((n_seq, rows, n_chan), F32), jax.ShapeDtypeStruct((n_seq, rows, n_skip), F32)),
+            out_shape=(jax.ShapeDtypeStruct((n_dev, TILE, n_chan), F32), jax.ShapeDtypeStruct((n_dev, TILE, n_skip), F32),
+                       jax.ShapeDtypeStruct((n_seq, rows, n_skip), F32)),
             in_specs=[any_spec] * 4,
-            out_specs=(vmem, vmem),
+            out_specs=[any_spec] * 3,
             scratch_shapes=[
                 pltpu.VMEM(w_in.shape, BF16), pltpu.VMEM(w_res.shape, BF16), pltpu.VMEM(w_skip.shape, BF16),
                 pltpu.VMEM(x.shape, BF16), pltpu.VMEM((n_seq, HALO, n_chan), BF16), pltpu.VMEM((n_seq, HALO, n_chan), BF16),
                 pltpu.VMEM((n_seq, rows + 2 * EDGE, n_chan), F32), pltpu.VMEM((n_seq, rows, n_skip), F32),
                 pltpu.VMEM((n_dev, TILE, n_chan), F32),
                 pltpu.VMEM((far_rows + 2 * pad, n_chan), F32), pltpu.VMEM((far_rows, n_skip), F32),
-                pltpu.VMEM((n_dev, TILE, n_chan), F32), pltpu.VMEM((n_dev, TILE, n_skip), F32),
-                pltpu.VMEM((m_max, 3 * n_chan), BF16), pltpu.VMEM((m_max, n_chan), BF16),
-                dma, dma((n_layers, 3)), dma((2,)), dma((2,)), dma((n_dev,)), dma((n_dev,)), dma((2, n_dev)), dma((2, n_dev)),
+                pltpu.VMEM((m_max, 3 * n_chan), BF16), pltpu.VMEM((m_max, n_chan), BF16), pltpu.VMEM((n_seq * rows, n_near * n_chan), BF16),
+                dma, dma((3,)), dma((n_layers, 3)), dma((2,)), dma((2,)), dma((n_dev,)), dma((n_dev,)), dma((2, n_dev)), dma((2, n_dev)),
             ],
             compiler_params=pltpu.CompilerParams(collective_id=0, has_side_effects=True, vmem_limit_bytes=63 * 2 ** 20),
             name='dilated_stack',
         )(x, w_in, w_res, w_skip)
+        blocks = lambda width: pl.BlockSpec((n_res, TILE, width), lambda i: (i, 0, 0))
+        whole = lambda width: pl.BlockSpec((1, rows, width), lambda i: (i, 0, 0))
+        return pl.pallas_call(
+            assemble_kernel,
+            grid=(n_seq,),
+            out_shape=(jax.ShapeDtypeStruct((n_seq, rows, n_chan), F32), jax.ShapeDtypeStruct((n_seq, rows, n_skip), F32)),
+            in_specs=[blocks(n_chan), blocks(n_skip), whole(n_skip)],
+            out_specs=(whole(n_chan), whole(n_skip)),
+            name='assemble',
+        )(home_h, home_s, skip)
 
     return jax.shard_map(local_stack, mesh=mesh, in_specs=(act_spec, P(), P(), P()), out_specs=(act_spec, act_spec), check_vma=False)

time: 69.4 us -> 55.9 us (0.81)
  Pallas kernels: 64.8 us -> 55.1 us
  local copies, waits for them, and re-layouts: 3.74 us -> 0 us
    pallas_call x1, Pallas kernels: 64.8 us -> 51.6 us  [local_stack(): pl.pallas_call(functools.partial(stack_kernel, n_dev, n_near), out_shape=...]
    unnamed x2 -> x0, local copies, waits for them, and re-layouts: 3.74 us -> none
    pallas_call x0 -> x1, Pallas kernels: none -> 3.54 us  [local_stack(): pl.pallas_call(assemble_kernel, grid=(n_seq,), out_shape=(jax.ShapeDtypeS...]
where the time goes in v2:
time: 55.9 us; the launch traced here: 55.8 us
  Pallas kernels  55.1 us (99%)
  between operations  0.64 us (1%)
    pallas_call x1, Pallas kernels, local_stack(): pl.pallas_call(functools.partial(stack_kernel, n_dev, n_near), out_shape=...  51.6 us
    pallas_call x1, Pallas kernels, local_stack(): pl.pallas_call(assemble_kernel, grid=(n_seq,), out_shape=(jax.ShapeDtypeS...  3.54 us

profile of v2, /device:TPU:97, one launch (start us, length us, event | category | flops | bytes accessed | tf_op | source)
XLA Modules:
  0.0 55.8 jit_solution(11861060677675405644)
XLA Ops:
  0.6 51.6 %dilated_stack.1 = (f32[32,8,512]{2,1,0:T(8,128)}, f32[32,8,512]{2,1,0:T(8,128)}, f32[4,64,512]{2,1,0:T(8,128)}) custom-call(bf16[4,64,512]{2,1,0:T(8,128)(2,1)} %x_hbm.1, bf16[11,3,512,1024]{3,2,1,0:T(8,128)(2,1)} %win_hbm.1, bf16[11,512,512]{2,1,0:T(8,128)(2,1)} %wres_hbm.1, bf16[11,512,512]{2,1,0:T(8,128)(2,1)} %wskip_hbm.1), custom_call_target="tpu_custom_call" | custom-call | tf_op jit(solution)/shard_map/dilated_stack/pallas_call | solution.py:235
  52.2 3.5 %assemble.1 = (f32[4,64,512]{2,1,0:T(8,128)}, f32[4,64,512]{2,1,0:T(8,128)}) custom-call(f32[32,8,512]{2,1,0:T(8,128)} %get-tuple-element.5.h_blocks, f32[32,8,512]{2,1,0:T(8,128)} %get-tuple-element.6.s_blocks, f32[4,64,512]{2,1,0:T(8,128)} %get-tuple-element.7.skip), custom_call_target="tpu_custom_call" | custom-call | tf_op jit(solution)/shard_map/assemble/pallas_call | solution.py:255

commit v3 on v2

--- a/solution.py
+++ b/solution.py
@@ -10,14 +10,15 @@
 MESH = pl.DeviceIdType.MESH
 F32, BF16 = jnp.float32, jnp.bfloat16
 TILE = 8
+ROW = 8
 HALO = 8
 EDGE = 16
 COLS = 256
 
 
-def stack_kernel(n_dev, n_near, x_hbm, win_hbm, wres_hbm, wskip_hbm, home_h, home_s, skip_out, win, wres, wskip, xv, halo_l, halo_r,
+def stack_kernel(n_dev, n_near, xv, win_hbm, wres_hbm, wskip_hbm, home_h, home_s, skip_out, win, wres, wskip, halo_l, halo_r,
                  near, near_skip, out_blocks, far, far_skip, lhs, gate, near_gate,
-                 x_sem, own_sem, w_sem, halo_send, halo_recv, mid_send, mid_recv, end_send, end_recv):
+                 own_sem, w_sem, halo_send, halo_recv, ready_sem, mid_send, mid_recv, end_send, end_recv):
     me = lax.axis_index('sp')
     n_seq, rows, n_chan = xv.shape
     n_skip = far_skip.shape[1]
@@ -27,14 +28,31 @@
     n_res = rows // TILE
     last = n_dev - 1
 
+    n_rows = n_dev // ROW
+    row, col = me // ROW, lax.rem(me, ROW)
     barrier = pltpu.get_barrier_semaphore()
 
-    @pl.loop(1, n_dev)
-    def _(k):
-        pl.semaphore_signal(barrier, inc=1, device_id={'sp': lax.rem(me + k, n_dev)}, device_id_type=MESH)
-
-    x_copy = pltpu.make_async_copy(x_hbm, xv, x_sem)
-    x_copy.start()
+    def tell(sem, dst):
+        pl.semaphore_signal(sem, inc=1, device_id={'sp': dst}, device_id_type=MESH)
+
+    for k in range(1, ROW):
+        tell(barrier, row * ROW + lax.rem(col + k, ROW))
+
+    def column(k):
+        return lax.rem(row + k, n_rows) * ROW + col
+
+    for k in range(1, n_rows):
+        tell(barrier, column(k))
+    before = jnp.logical_and(col == 0, row > 0)
+    after = jnp.logical_and(col == ROW - 1, row < n_rows - 1)
+
+    @pl.when(before)
+    def _():
+        tell(barrier, me - 1)
+
+    @pl.when(after)
+    def _():
+        tell(barrier, me + 1)
 
     def weight_copies(layer):
         return [pltpu.make_async_copy(win_hbm.at[layer], win.at[layer], w_sem.at[layer, 0]),
@@ -47,11 +65,11 @@
     far[:pad] = jnp.zeros((pad, n_chan), F32)
     far[pad + far_rows:] = jnp.zeros((pad, n_chan), F32)
 
-    x_copy.wait()
     for layer in range(n_near):
         for copy in weight_copies(layer):
             copy.start()
-    pl.semaphore_wait(barrier, n_dev - 1)
+    pl.semaphore_wait(barrier, ROW + n_rows - 2 + jnp.where(before, 1, 0) + jnp.where(after, 1, 0))
+
 
     def to_next():
         return pltpu.make_async_remote_copy(src_ref=xv.at[:, pl.ds(rows - HALO, HALO)], dst_ref=halo_l, send_sem=halo_send.at[0],
@@ -69,6 +87,8 @@
     def _():
         to_prev().start()
 
+    for k in range(1, n_rows):
+        tell(ready_sem, column(k))
     near[:, EDGE:EDGE + rows] = xv[...].astype(F32)
 
     @pl.when(me > 0)
@@ -129,7 +149,9 @@
 
     def mid_copy(dst, src):
         return pltpu.make_async_remote_copy(src_ref=out_blocks.at[dst], dst_ref=far.at[pl.ds(pl.multiple_of(pad + src * TILE, TILE), TILE)],
-                                            send_sem=mid_send.at[dst], recv_sem=mid_recv.at[src], device_id={'sp': dst}, device_id_type=MESH)
+                                            send_sem=mid_send, recv_sem=mid_recv, device_id={'sp': dst}, device_id_type=MESH)
+
+    pl.semaphore_wait(ready_sem, n_rows - 1)
 
     @pl.loop(1, n_dev)
     def _(k):
@@ -145,15 +167,13 @@
     skip_copy = pltpu.make_async_copy(near_skip, skip_out, own_sem.at[2])
     skip_copy.start()
 
-    @pl.loop(1, n_dev)
-    def _(k):
-        src = lax.rem(me + n_dev - k, n_dev)
-        mid_copy(lax.rem(me + k, n_dev), src).wait_recv()
+    others = pl.ds(0, n_dev - 1)
+    pltpu.make_async_copy(out_blocks.at[others], out_blocks.at[others], mid_recv).wait()
 
     def end_copy(which, dst, src):
         source = far.at[pl.ds(pl.multiple_of(pad + dst * TILE, TILE), TILE)] if which == 0 else far_skip.at[pl.ds(pl.multiple_of(dst * TILE, TILE), TILE)]
         return pltpu.make_async_remote_copy(src_ref=source, dst_ref=(home_h, home_s)[which].at[src],
-                                            send_sem=end_send.at[which, dst], recv_sem=end_recv.at[which, src], device_id={'sp': dst}, device_id_type=MESH)
+                                            send_sem=end_send.at[which], recv_sem=end_recv.at[which], device_id={'sp': dst}, device_id_type=MESH)
 
     def own_copy(which):
         source = far.at[pl.ds(pl.multiple_of(pad + me * TILE, TILE), TILE)] if which == 0 else far_skip.at[pl.ds(pl.multiple_of(me * TILE, TILE), TILE)]
@@ -187,11 +207,13 @@
 
     send_home(1)
 
+    pltpu.make_async_copy(out_blocks.at[others], out_blocks.at[others], mid_send).wait()
     for which in range(2):
-        @pl.loop(1, n_dev)
-        def _(k):
-            end_copy(which, lax.rem(me + k, n_dev), lax.rem(me + n_dev - k, n_dev)).wait_recv()
-
+        blocks = (home_h, home_s)[which].at[others]
+        pltpu.make_async_copy(blocks, blocks, end_recv.at[which]).wait()
+    for which in range(2):
+        blocks = (home_h, home_s)[which].at[others]
+        pltpu.make_async_copy(blocks, blocks, end_send.at[which]).wait()
     skip_copy.wait()
     own_copy(0).wait()
     own_copy(1).wait()
@@ -204,18 +226,24 @@
     def _():
         to_prev().wait_send()
 
-    @pl.loop(1, n_dev)
-    def _(k):
-        dst = lax.rem(me + k, n_dev)
-        mid_copy(dst, me).wait_send()
-        end_copy(0, dst, me).wait_send()
-        end_copy(1, dst, me).wait_send()
-
-
-def assemble_kernel(h_blocks, s_blocks, skip, h_out, s_out):
-    n_res = h_blocks.shape[0]
-    h_out[0] = jnp.swapaxes(h_blocks[...], 0, 1).reshape(h_out.shape[1:])
-    s_out[0] = jnp.swapaxes(s_blocks[...], 0, 1).reshape(s_out.shape[1:]) + skip[0]
+
+def assemble_kernel(h_blocks, s_blocks, skip, h_out, s_out, h_rows, s_rows, sems):
+    n_seq, rows, n_chan = h_rows.shape
+    n_res = h_blocks.shape[0] // n_seq
+
+    def copies(seq):
+        return (pltpu.make_async_copy(h_rows.at[seq], h_out.at[seq], sems.at[0, seq]),
+                pltpu.make_async_copy(s_rows.at[seq], s_out.at[seq], sems.at[1, seq]))
+
+    for seq in range(n_seq):
+        blocks = slice(seq * n_res, (seq + 1) * n_res)
+        h_rows[seq] = jnp.swapaxes(h_blocks[blocks], 0, 1).reshape(rows, n_chan)
+        copies(seq)[0].start()
+        s_rows[seq] = jnp.swapaxes(s_blocks[blocks], 0, 1).reshape(rows, s_rows.shape[2]) + skip[seq]
+        copies(seq)[1].start()
+    for seq in range(n_seq):
+        for copy in copies(seq):
+            copy.wait()
 
 
 def solution(mesh):
@@ -236,28 +264,27 @@
             functools.partial(stack_kernel, n_dev, n_near),
             out_shape=(jax.ShapeDtypeStruct((n_dev, TILE, n_chan), F32), jax.ShapeDtypeStruct((n_dev, TILE, n_skip), F32),
                        jax.ShapeDtypeStruct((n_seq, rows, n_skip), F32)),
-            in_specs=[any_spec] * 4,
+            in_specs=[pl.BlockSpec(memory_space=pltpu.VMEM)] + [any_spec] * 3,
             out_specs=[any_spec] * 3,
             scratch_shapes=[
                 pltpu.VMEM(w_in.shape, BF16), pltpu.VMEM(w_res.shape, BF16), pltpu.VMEM(w_skip.shape, BF16),
-                pltpu.VMEM(x.shape, BF16), pltpu.VMEM((n_seq, HALO, n_chan), BF16), pltpu.VMEM((n_seq, HALO, n_chan), BF16),
+                pltpu.VMEM((n_seq, HALO, n_chan), BF16), pltpu.VMEM((n_seq, HALO, n_chan), BF16),
                 pltpu.VMEM((n_seq, rows + 2 * EDGE, n_chan), F32), pltpu.VMEM((n_seq, rows, n_skip), F32),
                 pltpu.VMEM((n_dev, TILE, n_chan), F32),
                 pltpu.VMEM((far_rows + 2 * pad, n_chan), F32), pltpu.VMEM((far_rows, n_skip), F32),
                 pltpu.VMEM((m_max, 3 * n_chan), BF16), pltpu.VMEM((m_max, n_chan), BF16), pltpu.VMEM((n_seq * rows, n_near * n_chan), BF16),
-                dma, dma((3,)), dma((n_layers, 3)), dma((2,)), dma((2,)), dma((n_dev,)), dma((n_dev,)), dma((2, n_dev)), dma((2, n_dev)),
+                dma((3,)), dma((n_layers, 3)), dma((2,)), dma((2,)), pltpu.SemaphoreType.REGULAR, dma, dma, dma((2,)), dma((2,)),
             ],
-            compiler_params=pltpu.CompilerParams(collective_id=0, has_side_effects=True, vmem_limit_bytes=63 * 2 ** 20),
+            compiler_params=pltpu.CompilerParams(collective_id=0, has_side_effects=True, vmem_limit_bytes=52 * 2 ** 20),
             name='dilated_stack',
         )(x, w_in, w_res, w_skip)
-        blocks = lambda width: pl.BlockSpec((n_res, TILE, width), lambda i: (i, 0, 0))
-        whole = lambda width: pl.BlockSpec((1, rows, width), lambda i: (i, 0, 0))
         return pl.pallas_call(
             assemble_kernel,
-            grid=(n_seq,),
             out_shape=(jax.ShapeDtypeStruct((n_seq, rows, n_chan), F32), jax.ShapeDtypeStruct((n_seq, rows, n_skip), F32)),
-            in_specs=[blocks(n_chan), blocks(n_skip), whole(n_skip)],
-            out_specs=(whole(n_chan), whole(n_skip)),
+            in_specs=[pl.BlockSpec(memory_space=pltpu.VMEM)] * 3,
+            out_specs=[any_spec] * 2,
+            scratch_shapes=[pltpu.VMEM((n_seq, rows, n_chan), F32), pltpu.VMEM((n_seq, rows, n_skip), F32), dma((2, n_seq))],
+            compiler_params=pltpu.CompilerParams(vmem_limit_bytes=4 * 2 ** 20),
             name='assemble',
         )(home_h, home_s, skip)
 

time: 55.9 us -> 50.9 us (0.911)
  Pallas kernels: 55.1 us -> 49.2 us
  local copies, waits for them, and re-layouts: 0 us -> 0.94 us
    pallas_call x1, Pallas kernels: 51.6 us -> 48.1 us  [local_stack(): pl.pallas_call(functools.partial(stack_kernel, n_dev, n_near), out_shape=...]
    pallas_call x1, Pallas kernels: 3.54 us -> 1.05 us  [local_stack(): pl.pallas_call(assemble_kernel, out_shape=(jax.ShapeDtypeStruct((n_seq, r...]
    unnamed x0 -> x2, local copies, waits for them, and re-layouts: none -> 0.94 us
where the time goes in v3:
time: 50.9 us; the launch traced here: 50.7 us
  Pallas kernels  49.2 us (97%)
  local copies, waits for them, and re-layouts  0.94 us (2%)
  between operations  0.65 us (1%)
    pallas_call x1, Pallas kernels, local_stack(): pl.pallas_call(functools.partial(stack_kernel, n_dev, n_near), out_shape=...  48.1 us
    pallas_call x1, Pallas kernels, local_stack(): pl.pallas_call(assemble_kernel, out_shape=(jax.ShapeDtypeStruct((n_seq, r...  1.05 us

profile of v3, /device:TPU:97, one launch (start us, length us, event | category | flops | bytes accessed | tf_op | source)
XLA Modules:
  0.0 50.7 jit_solution(91290736102200478)
XLA Ops:
  0.6 0.0 copy-start
  0.6 0.9 %copy-done = bf16[4,64,512]{2,1,0:T(8,128)(2,1)S(1)} copy-done((bf16[4,64,512]{2,1,0:T(8,128)(2,1)S(1)}, bf16[4,64,512]{2,1,0:T(8,128)(2,1)}, u32[]{:S(2)}) %copy-start) | copy-done | bytes 262168
  1.6 48.1 %dilated_stack.1 = (f32[32,8,512]{2,1,0:T(8,128)S(1)}, f32[32,8,512]{2,1,0:T(8,128)S(1)}, f32[4,64,512]{2,1,0:T(8,128)S(1)}) custom-call(bf16[4,64,512]{2,1,0:T(8,128)(2,1)S(1)} %copy-done, bf16[11,3,512,1024]{3,2,1,0:T(8,128)(2,1)} %win_hbm.1, bf16[11,512,512]{2,1,0:T(8,128)(2,1)} %wres_hbm.1, bf16[11,512,512]{2,1,0:T(8,128)(2,1)} %wskip_hbm.1), custom_call_target="tpu_custom_call" | custom-call | tf_op jit(solution)/shard_map/dilated_stack/pallas_call | solution.py:263
  49.7 1.1 %assemble.1 = (f32[4,64,512]{2,1,0:T(8,128)}, f32[4,64,512]{2,1,0:T(8,128)}) custom-call(f32[32,8,512]{2,1,0:T(8,128)S(1)} %get-tuple-element.5.h_blocks, f32[32,8,512]{2,1,0:T(8,128)S(1)} %get-tuple-element.6.s_blocks, f32[4,64,512]{2,1,0:T(8,128)S(1)} %get-tuple-element.7.skip), custom_call_target="tpu_custom_call" | custom-call | tf_op jit(solution)/shard_map/assemble/pallas_call | solution.py:281
Async XLA Ops:
  0.6 1.0 %copy-start = (bf16[4,64,512]{2,1,0:T(8,128)(2,1)S(1)}, bf16[4,64,512]{2,1,0:T(8,128)(2,1)}, u32[]{:S(2)}) copy-start(bf16[4,64,512]{2,1,0:T(8,128)(2,1)} %xv.1) | copy-start | bytes 786436

commit v4 on v3

--- a/solution.py
+++ b/solution.py
@@ -10,6 +10,7 @@
 MESH = pl.DeviceIdType.MESH
 F32, BF16 = jnp.float32, jnp.bfloat16
 TILE = 8
+AHEAD = 3
 ROW = 8
 HALO = 8
 EDGE = 16
@@ -28,36 +29,57 @@
     n_res = rows // TILE
     last = n_dev - 1
 
-    n_rows = n_dev // ROW
-    row, col = me // ROW, lax.rem(me, ROW)
-    barrier = pltpu.get_barrier_semaphore()
-
-    def tell(sem, dst):
-        pl.semaphore_signal(sem, inc=1, device_id={'sp': dst}, device_id_type=MESH)
-
-    for k in range(1, ROW):
-        tell(barrier, row * ROW + lax.rem(col + k, ROW))
-
-    def column(k):
-        return lax.rem(row + k, n_rows) * ROW + col
-
-    for k in range(1, n_rows):
-        tell(barrier, column(k))
-    before = jnp.logical_and(col == 0, row > 0)
-    after = jnp.logical_and(col == ROW - 1, row < n_rows - 1)
-
-    @pl.when(before)
-    def _():
-        tell(barrier, me - 1)
-
-    @pl.when(after)
-    def _():
-        tell(barrier, me + 1)
-
     def weight_copies(layer):
         return [pltpu.make_async_copy(win_hbm.at[layer], win.at[layer], w_sem.at[layer, 0]),
                 pltpu.make_async_copy(wres_hbm.at[layer], wres.at[layer], w_sem.at[layer, 1]),
                 pltpu.make_async_copy(wskip_hbm.at[layer], wskip.at[layer], w_sem.at[layer, 2])]
+
+    def start_weights(*layers):
+        for layer in layers:
+            for copy in weight_copies(layer):
+                copy.start()
+
+    start_weights(0)
+
+    n_rows = n_dev // ROW
+    row, col = me // ROW, lax.rem(me, ROW)
+    barrier = pltpu.get_barrier_semaphore()
+
+    def tell(sem, dst):
+        pl.semaphore_signal(sem, inc=1, device_id={'sp': dst}, device_id_type=MESH)
+
+    for k in range(1, ROW):
+        tell(barrier, row * ROW + lax.rem(col + k, ROW))
+
+    up, down = row > 0, row < n_rows - 1
+
+    def tell_column(sem):
+        @pl.when(up)
+        def _():
+            tell(sem, me - ROW)
+
+        @pl.when(down)
+        def _():
+            tell(sem, me + ROW)
+
+    tell_column(barrier)
+    before, after = jnp.logical_and(col == 0, up), jnp.logical_and(col == ROW - 1, down)
+
+    @pl.when(before)
+    def _():
+        tell(barrier, me - 1)
+
+    @pl.when(after)
+    def _():
+        tell(barrier, me + 1)
+
+    def count(*conditions):
+        return sum(jnp.where(c, 1, 0) for c in conditions)
+
+    def heard_column(step):
+        pl.semaphore_wait(ready_sem.at[step - 1], count(up, down))
+        if step < n_rows - 1:
+            tell_column(ready_sem.at[step])
 
     zero_edge = jnp.zeros((n_seq, EDGE, n_chan), F32)
     near[:, :EDGE] = zero_edge
@@ -65,10 +87,9 @@
     far[:pad] = jnp.zeros((pad, n_chan), F32)
     far[pad + far_rows:] = jnp.zeros((pad, n_chan), F32)
 
-    for layer in range(n_near):
-        for copy in weight_copies(layer):
-            copy.start()
-    pl.semaphore_wait(barrier, ROW + n_rows - 2 + jnp.where(before, 1, 0) + jnp.where(after, 1, 0))
+    pl.semaphore_wait(barrier, ROW - 1 + count(up, down, before, after))
+    tell_column(ready_sem.at[0])
+    start_weights(*range(1, n_near))
 
 
     def to_next():
@@ -87,8 +108,6 @@
     def _():
         to_prev().start()
 
-    for k in range(1, n_rows):
-        tell(ready_sem, column(k))
     near[:, EDGE:EDGE + rows] = xv[...].astype(F32)
 
     @pl.when(me > 0)
@@ -123,10 +142,10 @@
                 lhs[seq * size:(seq + 1) * size, tap * n_chan:(tap + 1) * n_chan] = near[seq, off:off + size].astype(BF16)
         for copy in weight_copies(layer):
             copy.wait()
+        if layer == n_near - 2:
+            start_weights(*range(n_near, n_near + AHEAD))
         if layer == n_near - 1:
-            for later in range(n_near, n_layers):
-                for copy in weight_copies(later):
-                    copy.start()
+            start_weights(*range(n_near + AHEAD, n_layers))
         gated_layer(layer, m)
         for seq in range(n_seq):
             begin = seq * size + EDGE - lo
@@ -135,6 +154,9 @@
             res = jnp.dot(gate[:m], wres[layer, :, col:col + COLS], preferred_element_type=F32).reshape(n_seq, size, COLS)
             near[:, lo:hi, col:col + COLS] = near[:, lo:hi, col:col + COLS] + res
         if layer < n_near - 1:
+            if layer + 1 < n_rows:
+                heard_column(layer + 1)
+
             @pl.when(me == 0)
             def _():
                 near[:, :EDGE] = zero_edge
@@ -151,7 +173,8 @@
         return pltpu.make_async_remote_copy(src_ref=out_blocks.at[dst], dst_ref=far.at[pl.ds(pl.multiple_of(pad + src * TILE, TILE), TILE)],
                                             send_sem=mid_send, recv_sem=mid_recv, device_id={'sp': dst}, device_id_type=MESH)
 
-    pl.semaphore_wait(ready_sem, n_rows - 1)
+    for step in range(n_near, n_rows):
+        heard_column(step)
 
     @pl.loop(1, n_dev)
     def _(k):
@@ -167,6 +190,9 @@
     skip_copy = pltpu.make_async_copy(near_skip, skip_out, own_sem.at[2])
     skip_copy.start()
 
+    for layer in range(n_near, n_layers):
+        for copy in weight_copies(layer):
+            copy.wait()
     others = pl.ds(0, n_dev - 1)
     pltpu.make_async_copy(out_blocks.at[others], out_blocks.at[others], mid_recv).wait()
 
@@ -180,9 +206,13 @@
         return pltpu.make_async_copy(source, (home_h, home_s)[which].at[me], own_sem.at[which])
 
     def send_home(which):
-        @pl.loop(1, n_dev)
+        @pl.loop(0, n_dev)
         def _(k):
-            end_copy(which, lax.rem(me + k, n_dev), me).start()
+            dst = k + 1 - 2 * lax.rem(k, 2)
+
+            @pl.when(dst != me)
+            def _():
+                end_copy(which, dst, me).start()
 
         own_copy(which).start()
 
@@ -191,8 +221,6 @@
         for tap in range(3):
             off = pad + (tap - 1) * dist
             lhs[:far_rows, tap * n_chan:(tap + 1) * n_chan] = far[off:off + far_rows].astype(BF16)
-        for copy in weight_copies(layer):
-            copy.wait()
         gated_layer(layer, far_rows)
         for col in range(0, n_chan, COLS):
             res = jnp.dot(gate[:far_rows], wres[layer, :, col:col + COLS], preferred_element_type=F32)
@@ -273,7 +301,7 @@
                 pltpu.VMEM((n_dev, TILE, n_chan), F32),
                 pltpu.VMEM((far_rows + 2 * pad, n_chan), F32), pltpu.VMEM((far_rows, n_skip), F32),
                 pltpu.VMEM((m_max, 3 * n_chan), BF16), pltpu.VMEM((m_max, n_chan), BF16), pltpu.VMEM((n_seq * rows, n_near * n_chan), BF16),
-                dma((3,)), dma((n_layers, 3)), dma((2,)), dma((2,)), pltpu.SemaphoreType.REGULAR, dma, dma, dma((2,)), dma((2,)),
+                dma((3,)), dma((n_layers, 3)), dma((2,)), dma((2,)), pltpu.SemaphoreType.REGULAR((max(n_dev // ROW - 1, 1),)), dma, dma, dma((2,)), dma((2,)),
             ],
             compiler_params=pltpu.CompilerParams(collective_id=0, has_side_effects=True, vmem_limit_bytes=52 * 2 ** 20),
             name='dilated_stack',

time: 50.9 us -> 48.3 us (0.949)
  Pallas kernels: 49.2 us -> 46.6 us
    pallas_call x1, Pallas kernels: 48.1 us -> 45.6 us  [local_stack(): pl.pallas_call(functools.partial(stack_kernel, n_dev, n_near), out_shape=...]
where the time goes in v4:
time: 48.3 us; the launch traced here: 48.2 us
  Pallas kernels  46.6 us (96%)
  local copies, waits for them, and re-layouts  0.94 us (2%)
  between operations  0.65 us (1%)
    pallas_call x1, Pallas kernels, local_stack(): pl.pallas_call(functools.partial(stack_kernel, n_dev, n_near), out_shape=...  45.6 us
    pallas_call x1, Pallas kernels, local_stack(): pl.pallas_call(assemble_kernel, out_shape=(jax.ShapeDtypeStruct((n_seq, r...  1.05 us

profile of v4, /device:TPU:97, one launch (start us, length us, event | category | flops | bytes accessed | tf_op | source)
XLA Modules:
  0.0 48.2 jit_solution(3705308524226502504)
XLA Ops:
  0.6 0.0 copy-start
  0.6 0.9 %copy-done = bf16[4,64,512]{2,1,0:T(8,128)(2,1)S(1)} copy-done((bf16[4,64,512]{2,1,0:T(8,128)(2,1)S(1)}, bf16[4,64,512]{2,1,0:T(8,128)(2,1)}, u32[]{:S(2)}) %copy-start) | copy-done | bytes 262168
  1.6 45.6 %dilated_stack.1 = (f32[32,8,512]{2,1,0:T(8,128)S(1)}, f32[32,8,512]{2,1,0:T(8,128)S(1)}, f32[4,64,512]{2,1,0:T(8,128)S(1)}) custom-call(bf16[4,64,512]{2,1,0:T(8,128)(2,1)S(1)} %copy-done, bf16[11,3,512,1024]{3,2,1,0:T(8,128)(2,1)} %win_hbm.1, bf16[11,512,512]{2,1,0:T(8,128)(2,1)} %wres_hbm.1, bf16[11,512,512]{2,1,0:T(8,128)(2,1)} %wskip_hbm.1), custom_call_target="tpu_custom_call" | custom-call | tf_op jit(solution)/shard_map/dilated_stack/pallas_call | solution.py:291
  47.2 1.1 %assemble.1 = (f32[4,64,512]{2,1,0:T(8,128)}, f32[4,64,512]{2,1,0:T(8,128)}) custom-call(f32[32,8,512]{2,1,0:T(8,128)S(1)} %get-tuple-element.5.h_blocks, f32[32,8,512]{2,1,0:T(8,128)S(1)} %get-tuple-element.6.s_blocks, f32[4,64,512]{2,1,0:T(8,128)S(1)} %get-tuple-element.7.skip), custom_call_target="tpu_custom_call" | custom-call | tf_op jit(solution)/shard_map/assemble/pallas_call | solution.py:309
Async XLA Ops:
  0.6 1.0 %copy-start = (bf16[4,64,512]{2,1,0:T(8,128)(2,1)S(1)}, bf16[4,64,512]{2,1,0:T(8,128)(2,1)}, u32[]{:S(2)}) copy-start(bf16[4,64,512]{2,1,0:T(8,128)(2,1)} %xv.1) | copy-start | bytes 786436

commit v5 on v4

v5 whole, which is shorter than its diff:
```python
import functools

import jax
import jax.numpy as jnp
from jax import lax
from jax.experimental import pallas as pl
from jax.experimental.pallas import tpu as pltpu
from jax.sharding import PartitionSpec as P

MESH = pl.DeviceIdType.MESH
F32, BF16 = jnp.float32, jnp.bfloat16
TILE = 8
AHEAD = 3
ROW = 8
HALO = 16
EDGE = 24
GROUPS = 2
COLS = 256


def swap_halves(first, second):
    half = first.shape[1] // 2
    upper = lax.broadcasted_iota(jnp.int32, first.shape, 1) < half
    return jnp.where(upper, first, pltpu.roll(second, half, 1)), jnp.where(upper, pltpu.roll(first, half, 1), second)


def stack_kernel(n_dev, n_near, xv, win_hbm, wres_hbm, wskip_hbm, home, skip_out, win, wres, wskip, halo_l, halo_r,
                 near, near_skip, mid_out, mid_in, far, far_skip, end_out, lhs, gate, near_gate,
                 own_sem, w_sem, halo_send, halo_recv, ready_sem, mid_send, mid_recv, end_send, end_recv):
    me = lax.axis_index('sp')
    n_seq, rows, n_chan = xv.shape
    n_skip = far_skip.shape[2]
    n_layers = win.shape[0]
    far_rows = far_skip.shape[1]
    pad = (far.shape[1] - far_rows) // 2
    in_group = n_seq // GROUPS
    n_res = n_dev // in_group
    part = rows // n_res
    lanes = n_chan * part // TILE
    n_side = TILE // part
    last = n_dev - 1

    def weight_copies(layer):
        return [pltpu.make_async_copy(win_hbm.at[layer], win.at[layer], w_sem.at[layer, 0]),
                pltpu.make_async_copy(wres_hbm.at[layer], wres.at[layer], w_sem.at[layer, 1]),
                pltpu.make_async_copy(wskip_hbm.at[layer], wskip.at[layer], w_sem.at[layer, 2])]

    def start_weights(*layers):
        for layer in layers:
            for copy in weight_copies(layer):
                copy.start()

    start_weights(0)

    n_rows = n_dev // ROW
    row, col = me // ROW, lax.rem(me, ROW)
    barrier = pltpu.get_barrier_semaphore()

    def tell(sem, dst):
        pl.semaphore_signal(sem, inc=1, device_id={'sp': dst}, device_id_type=MESH)

    for k in range(1, ROW):
        tell(barrier, row * ROW + lax.rem(col + k, ROW))

    up, down = row > 0, row < n_rows - 1

    def tell_column(sem):
        @pl.when(up)
        def _():
            tell(sem, me - ROW)

        @pl.when(down)
        def _():
            tell(sem, me + ROW)

    tell_column(barrier)
    before, after = jnp.logical_and(col == 0, up), jnp.logical_and(col == ROW - 1, down)

    @pl.when(before)
    def _():
        tell(barrier, me - 1)

    @pl.when(after)
    def _():
        tell(barrier, me + 1)

    def count(*conditions):
        return sum(jnp.where(c, 1, 0) for c in conditions)

    def heard_column(step):
        pl.semaphore_wait(ready_sem.at[step - 1], count(up, down))
        if step < n_rows - 1:
            tell_column(ready_sem.at[step])

    zero_edge = jnp.zeros((n_seq, EDGE, n_chan), F32)
    near[:, :EDGE] = zero_edge
    near[:, EDGE + rows:] = zero_edge
    for group in range(GROUPS):
        far[group, :pad] = jnp.zeros((pad, n_chan), F32)
        far[group, pad + far_rows:] = jnp.zeros((pad, n_chan), F32)

    pl.semaphore_wait(barrier, ROW - 1 + count(up, down, before, after))
    tell_column(ready_sem.at[0])
    start_weights(*range(1, n_near - 1))


    def to_next():
        return pltpu.make_async_remote_copy(src_ref=xv.at[:, pl.ds(rows - HALO, HALO)], dst_ref=halo_l, send_sem=halo_send.at[0],
                                            recv_sem=halo_recv.at[0], device_id={'sp': me + 1}, device_id_type=MESH)

    def to_prev():
        return pltpu.make_async_remote_copy(src_ref=xv.at[:, pl.ds(0, HALO)], dst_ref=halo_r, send_sem=halo_send.at[1],
                                            recv_sem=halo_recv.at[1], device_id={'sp': me - 1}, device_id_type=MESH)

    @pl.when(me < last)
    def _():
        to_next().start()

    @pl.when(me > 0)
    def _():
        to_prev().start()

    near[:, EDGE:EDGE + rows] = xv[...].astype(F32)

    @pl.when(me > 0)
    def _():
        to_next().wait_recv()
        near[:, EDGE - HALO:EDGE] = halo_l[...].astype(F32)

    @pl.when(me < last)
    def _():
        to_prev().wait_recv()
        near[:, EDGE + rows:EDGE + rows + HALO] = halo_r[...].astype(F32)

    def gated_layer(layer, m):
        w = win.at[layer]
        for col in range(0, n_chan, COLS):
            f = jnp.zeros((m, COLS), F32)
            g = jnp.zeros((m, COLS), F32)
            for tap in range(3):
                op = lhs[:m, tap * n_chan:(tap + 1) * n_chan]
                f = f + jnp.dot(op, w[tap, :, col:col + COLS], preferred_element_type=F32)
                g = g + jnp.dot(op, w[tap, :, n_chan + col:n_chan + col + COLS], preferred_element_type=F32)
            gate[:m, col:col + COLS] = (jnp.tanh(f) * (0.5 * jnp.tanh(0.5 * g) + 0.5)).astype(BF16)

    start_weights(n_near - 1)

    def near_phase(group):
        seqs = range(group * in_group, (group + 1) * in_group)
        every = slice(group * in_group, (group + 1) * in_group)
        for layer in range(n_near):
            dist = 2 ** layer
            reach = -(-(2 ** n_near - 2 * dist) // TILE) * TILE
            lo, hi = EDGE - reach, EDGE + rows + reach
            size = hi - lo
            m = in_group * size
            for tap in range(3):
                off = lo + (tap - 1) * dist
                for at, seq in enumerate(seqs):
                    lhs[at * size:(at + 1) * size, tap * n_chan:(tap + 1) * n_chan] = near[seq, off:off + size].astype(BF16)
            if group == 0:
                for copy in weight_copies(layer):
                    copy.wait()
                if layer == 1:
                    start_weights(*range(n_near, n_near + AHEAD))
                if layer == n_near - 1:
                    start_weights(*range(n_near + AHEAD, n_layers))
            gated_layer(layer, m)
            for at, seq in enumerate(seqs):
                begin = at * size + EDGE - lo
                near_gate[seq * rows:(seq + 1) * rows, layer * n_chan:(layer + 1) * n_chan] = gate[begin:begin + rows]
            for col in range(0, n_chan, COLS):
                res = jnp.dot(gate[:m], wres[layer, :, col:col + COLS], preferred_element_type=F32).reshape(in_group, size, COLS)
                near[every, lo:hi, col:col + COLS] = near[every, lo:hi, col:col + COLS] + res
            if group == 0 and layer + 1 < n_rows:
                heard_column(layer + 1)
            if layer < n_near - 1:
                @pl.when(me == 0)
                def _():
                    near[every, :EDGE] = zero_edge[:in_group]

                @pl.when(me == last)
                def _():
                    near[every, EDGE + rows:] = zero_edge[:in_group]

        for at, seq in enumerate(seqs):
            for low in range(0, n_res, TILE):
                sides = [near[seq, EDGE:EDGE + rows, side * lanes:(side + 1) * lanes].reshape(part, n_res, lanes)[:, low:low + TILE]
                         for side in range(n_side)]
                mid_out[group, at * n_res + low:at * n_res + low + TILE] = jnp.swapaxes(jnp.concatenate(sides, axis=0), 0, 1)

    def mid_copy(group, dst):
        return pltpu.make_async_remote_copy(src_ref=mid_out.at[group, dst], dst_ref=mid_in.at[group, me], send_sem=mid_send.at[group],
                                            recv_sem=mid_recv.at[group], device_id={'sp': dst}, device_id_type=MESH)

    def send_mid(group):
        @pl.loop(1, n_dev)
        def _(k):
            mid_copy(group, lax.rem(me + k, n_dev)).start()

        mid_in[group, me] = mid_out[group, me]

    for group in range(GROUPS):
        near_phase(group)
        if group == 0:
            for step in range(n_near + 1, n_rows):
                heard_column(step)
        send_mid(group)

    for col in range(0, n_skip, COLS):
        skip = jnp.zeros((n_seq * rows, COLS), F32)
        for layer in range(n_near):
            skip = skip + jnp.dot(near_gate[:, layer * n_chan:(layer + 1) * n_chan], wskip[layer, :, col:col + COLS], preferred_element_type=F32)
        near_skip[:, :, col:col + COLS] = skip.reshape(n_seq, rows, COLS)
    skip_copy = pltpu.make_async_copy(near_skip, skip_out, own_sem.at[GROUPS])
    skip_copy.start()

    def end_copy(group, dst):
        return pltpu.make_async_remote_copy(src_ref=end_out.at[group, dst // 2, lax.rem(dst, 2)], dst_ref=home.at[group, me],
                                            send_sem=end_send.at[group], recv_sem=end_recv.at[group], device_id={'sp': dst}, device_id_type=MESH)

    def own_copy(group):
        return pltpu.make_async_copy(end_out.at[group, me // 2, lax.rem(me, 2)], home.at[group, me], own_sem.at[group])

    def send_home(group):
        @pl.loop(0, n_dev)
        def _(k):
            dst = k + 1 - 2 * lax.rem(k, 2)

            @pl.when(dst != me)
            def _():
                end_copy(group, dst).start()

        own_copy(group).start()

    others = pl.ds(0, n_dev - 1)

    def wait_all(ref, sem):
        pltpu.make_async_copy(ref.at[others], ref.at[others], sem).wait()

    for group in range(GROUPS):
        wait_all(mid_in.at[group], mid_recv.at[group])
        blocks = mid_in[group].reshape(n_dev // 2, 2, TILE, lanes)
        for side, value in enumerate(swap_halves(blocks[:, 0], blocks[:, 1])):
            far[group, pad:pad + far_rows, side * lanes:(side + 1) * lanes] = value.reshape(far_rows, lanes)
        for layer in range(n_near, n_layers):
            dist = 2 ** layer // n_res
            for tap in range(3):
                off = pad + (tap - 1) * dist
                lhs[:far_rows, tap * n_chan:(tap + 1) * n_chan] = far[group, off:off + far_rows].astype(BF16)
            if group == 0:
                for copy in weight_copies(layer):
                    copy.wait()
            gated_layer(layer, far_rows)
            for col in range(0, n_chan, COLS):
                res = jnp.dot(gate[:far_rows], wres[layer, :, col:col + COLS], preferred_element_type=F32)
                far[group, pad:pad + far_rows, col:col + COLS] = far[group, pad:pad + far_rows, col:col + COLS] + res
            for col in range(0, n_skip, COLS):
                skip = jnp.dot(gate[:far_rows], wskip[layer, :, col:col + COLS], preferred_element_type=F32)
                if layer > n_near:
                    skip = far_skip[group, :, col:col + COLS] + skip
                far_skip[group, :, col:col + COLS] = skip
        for which, value in enumerate((far[group, pad:pad + far_rows], far_skip[group])):
            sides = [value[:, side * lanes:(side + 1) * lanes].reshape(n_dev // 2, TILE, lanes) for side in range(n_side)]
            for at, block in enumerate(swap_halves(*sides)):
                end_out[group, :, at, which * TILE:(which + 1) * TILE] = block
        send_home(group)

    for group in range(GROUPS):
        wait_all(mid_out.at[group], mid_send.at[group])
    for group in range(GROUPS):
        wait_all(home.at[group], end_recv.at[group])
    for group in range(GROUPS):
        wait_all(home.at[group], end_send.at[group])
        own_copy(group).wait()
    skip_copy.wait()

    @pl.when(me < last)
    def _():
        to_next().wait_send()

    @pl.when(me > 0)
    def _():
        to_prev().wait_send()


def assemble_kernel(home, skip, h_out, s_out, h_rows, s_rows, sems):
    n_seq, rows, n_chan = h_rows.shape
    lanes = home.shape[3]
    in_group = n_seq // GROUPS
    n_res = home.shape[1] // in_group
    part = rows // n_res

    def copies(seq):
        return (pltpu.make_async_copy(h_rows.at[seq], h_out.at[seq], sems.at[0, seq]),
                pltpu.make_async_copy(s_rows.at[seq], s_out.at[seq], sems.at[1, seq]))

    for seq in range(n_seq):
        group, at = seq // in_group, seq % in_group
        for which, out in enumerate((h_rows, s_rows)):
            for low in range(0, n_res, TILE):
                blocks = home[group, at * n_res + low:at * n_res + low + TILE, which * TILE:(which + 1) * TILE]
                turned = jnp.swapaxes(blocks, 0, 1)
                for k in range(TILE):
                    begin, side = k % part * n_res + low, k // part
                    value = turned[k]
                    if which == 1:
                        value = value + skip[seq, begin:begin + TILE, side * lanes:(side + 1) * lanes]
                    out[seq, begin:begin + TILE, side * lanes:(side + 1) * lanes] = value
            copies(seq)[which].start()
    for seq in range(n_seq):
        for copy in copies(seq):
            copy.wait()


def solution(mesh):
    n_dev = mesh.shape['sp']
    act_spec = P('dp', 'sp', None)

    def local_stack(x, w_in, w_res, w_skip):
        n_seq, rows, n_chan = x.shape
        n_layers, n_skip = w_in.shape[0], w_skip.shape[2]
        n_res = n_dev * GROUPS // n_seq
        n_near = n_res.bit_length() - 1
        far_rows = n_dev * rows // n_res
        pad = 2 ** (n_layers - 1) // n_res
        part = rows // n_res
        lanes = n_chan * part // TILE
        assert TILE == 2 * part and n_skip == n_chan
        any_spec = pl.BlockSpec(memory_space=pl.ANY)
        m_max = n_seq // GROUPS * (rows + 2 * HALO)
        dma = pltpu.SemaphoreType.DMA
        home, skip = pl.pallas_call(
            functools.partial(stack_kernel, n_dev, n_near),
            out_shape=(jax.ShapeDtypeStruct((GROUPS, n_dev, 2 * TILE, lanes), F32), jax.ShapeDtypeStruct((n_seq, rows, n_skip), F32)),
            in_specs=[pl.BlockSpec(memory_space=pltpu.VMEM)] + [any_spec] * 3,
            out_specs=[any_spec] * 2,
            scratch_shapes=[
                pltpu.VMEM(w_in.shape, BF16), pltpu.VMEM(w_res.shape, BF16), pltpu.VMEM(w_skip.shape, BF16),
                pltpu.VMEM((n_seq, HALO, n_chan), BF16), pltpu.VMEM((n_seq, HALO, n_chan), BF16),
                pltpu.VMEM((n_seq, rows + 2 * EDGE, n_chan), F32), pltpu.VMEM((n_seq, rows, n_skip), F32),
                pltpu.VMEM((GROUPS, n_dev, TILE, lanes), F32), pltpu.VMEM((GROUPS, n_dev, TILE, lanes), F32),
                pltpu.VMEM((GROUPS, far_rows + 2 * pad, n_chan), F32), pltpu.VMEM((GROUPS, far_rows, n_skip), F32),
                pltpu.VMEM((GROUPS, n_dev // 2, 2, 2 * TILE, lanes), F32),
                pltpu.VMEM((m_max, 3 * n_chan), BF16), pltpu.VMEM((m_max, n_chan), BF16), pltpu.VMEM((n_seq * rows, n_near * n_chan), BF16),
                dma((GROUPS + 1,)), dma((n_layers, 3)), dma((2,)), dma((2,)), pltpu.SemaphoreType.REGULAR((max(n_dev // ROW - 1, 1),)), *[dma((GROUPS,)) for _ in range(4)],
            ],
            compiler_params=pltpu.CompilerParams(collective_id=0, has_side_effects=True, vmem_limit_bytes=52 * 2 ** 20),
            name='dilated_stack',
        )(x, w_in, w_res, w_skip)
        return pl.pallas_call(
            assemble_kernel,
            out_shape=(jax.ShapeDtypeStruct((n_seq, rows, n_chan), F32), jax.ShapeDtypeStruct((n_seq, rows, n_skip), F32)),
            in_specs=[pl.BlockSpec(memory_space=pltpu.VMEM)] * 2,
            out_specs=[any_spec] * 2,
            scratch_shapes=[pltpu.VMEM((n_seq, rows, n_chan), F32), pltpu.VMEM((n_seq, rows, n_skip), F32), dma((2, n_seq))],
            compiler_params=pltpu.CompilerParams(vmem_limit_bytes=4 * 2 ** 20),
            name='assemble',
        )(home, skip)

    return jax.shard_map(local_stack, mesh=mesh, in_specs=(act_spec, P(), P(), P()), out_specs=(act_spec, act_spec), check_vma=False)
```

time: 48.3 us -> 43 us (0.89)
  Pallas kernels: 46.6 us -> 41.1 us
    pallas_call x1, Pallas kernels: 45.6 us -> 40.1 us  [local_stack(): pl.pallas_call(functools.partial(stack_kernel, n_dev, n_near), out_shape=...]
where the time goes in v5:
time: 43 us; the launch traced here: 42.9 us
  Pallas kernels  41.1 us (96%)
  local copies, waits for them, and re-layouts  0.94 us (2%)
  between operations  0.81 us (2%)
    pallas_call x1, Pallas kernels, local_stack(): pl.pallas_call(functools.partial(stack_kernel, n_dev, n_near), out_shape=...  40.1 us
    pallas_call x1, Pallas kernels, local_stack(): pl.pallas_call(assemble_kernel, out_shape=(jax.ShapeDtypeStruct((n_seq, r...  1.05 us
    unnamed x2, local copies, waits for them, and re-layouts  0.94 us

profile of v5, /device:TPU:97, one launch (start us, length us, event | category | flops | bytes accessed | tf_op | source)
XLA Modules:
  0.0 42.9 jit_solution(14663670984843642178)
XLA Ops:
  0.6 0.0 copy-start
  0.6 0.9 %copy-done = bf16[4,64,512]{2,1,0:T(8,128)(2,1)S(1)} copy-done((bf16[4,64,512]{2,1,0:T(8,128)(2,1)S(1)}, bf16[4,64,512]{2,1,0:T(8,128)(2,1)}, u32[]{:S(2)}) %copy-start) | copy-done | bytes 262168
  1.6 40.1 %dilated_stack.1 = (f32[2,32,16,256]{3,2,1,0:T(8,128)S(1)}, f32[4,64,512]{2,1,0:T(8,128)S(1)}) custom-call(bf16[4,64,512]{2,1,0:T(8,128)(2,1)S(1)} %copy-done, bf16[11,3,512,1024]{3,2,1,0:T(8,128)(2,1)} %win_hbm.1, bf16[11,512,512]{2,1,0:T(8,128)(2,1)} %wres_hbm.1, bf16[11,512,512]{2,1,0:T(8,128)(2,1)} %wskip_hbm.1), custom_call_target="tpu_custom_call" | custom-call | tf_op jit(solution)/shard_map/dilated_stack/pallas_call | solution.py:333
  41.7 1.1 %assemble.1 = (f32[4,64,512]{2,1,0:T(8,128)}, f32[4,64,512]{2,1,0:T(8,128)}) custom-call(f32[2,32,16,256]{3,2,1,0:T(8,128)S(1)} %get-tuple-element.4.home, f32[4,64,512]{2,1,0:T(8,128)S(1)} %get-tuple-element.5.skip), custom_call_target="tpu_custom_call" | custom-call | tf_op jit(solution)/shard_map/assemble/pallas_call | solution.py:351
Async XLA Ops:
  0.6 1.0 %copy-start = (bf16[4,64,512]{2,1,0:T(8,128)(2,1)S(1)}, bf16[4,64,512]{2,1,0:T(8,128)(2,1)}, u32[]{:S(2)}) copy-start(bf16[4,64,512]{2,1,0:T(8,128)(2,1)} %xv.1) | copy-start | bytes 786436

commit v6 on v5

--- a/solution.py
+++ b/solution.py
@@ -11,6 +11,7 @@
 F32, BF16 = jnp.float32, jnp.bfloat16
 TILE = 8
 AHEAD = 3
+UNROLL = 31
 ROW = 8
 HALO = 16
 EDGE = 24
@@ -104,33 +105,44 @@
     start_weights(*range(1, n_near - 1))
 
 
-    def to_next():
-        return pltpu.make_async_remote_copy(src_ref=xv.at[:, pl.ds(rows - HALO, HALO)], dst_ref=halo_l, send_sem=halo_send.at[0],
-                                            recv_sem=halo_recv.at[0], device_id={'sp': me + 1}, device_id_type=MESH)
-
-    def to_prev():
-        return pltpu.make_async_remote_copy(src_ref=xv.at[:, pl.ds(0, HALO)], dst_ref=halo_r, send_sem=halo_send.at[1],
-                                            recv_sem=halo_recv.at[1], device_id={'sp': me - 1}, device_id_type=MESH)
-
-    @pl.when(me < last)
-    def _():
-        to_next().start()
-
-    @pl.when(me > 0)
-    def _():
-        to_prev().start()
+    def seqs_of(group):
+        return pl.ds(group * in_group, in_group)
+
+    def to_next(group):
+        return pltpu.make_async_remote_copy(src_ref=xv.at[seqs_of(group), pl.ds(rows - HALO, HALO)], dst_ref=halo_l.at[seqs_of(group)],
+                                            send_sem=halo_send.at[0, group], recv_sem=halo_recv.at[0, group],
+                                            device_id={'sp': me + 1}, device_id_type=MESH)
+
+    def to_prev(group):
+        return pltpu.make_async_remote_copy(src_ref=xv.at[seqs_of(group), pl.ds(0, HALO)], dst_ref=halo_r.at[seqs_of(group)],
+                                            send_sem=halo_send.at[1, group], recv_sem=halo_recv.at[1, group],
+                                            device_id={'sp': me - 1}, device_id_type=MESH)
+
+    for group in range(GROUPS):
+        @pl.when(me < last)
+        def _():
+            to_next(group).start()
+
+        @pl.when(me > 0)
+        def _():
+            to_prev(group).start()
 
     near[:, EDGE:EDGE + rows] = xv[...].astype(F32)
-
-    @pl.when(me > 0)
-    def _():
-        to_next().wait_recv()
-        near[:, EDGE - HALO:EDGE] = halo_l[...].astype(F32)
-
-    @pl.when(me < last)
-    def _():
-        to_prev().wait_recv()
-        near[:, EDGE + rows:EDGE + rows + HALO] = halo_r[...].astype(F32)
+    if n_rows > 1:
+        heard_column(1)
+
+    def take_halo(group):
+        every = slice(group * in_group, (group + 1) * in_group)
+
+        @pl.when(me > 0)
+        def _():
+            to_next(group).wait_recv()
+            near[every, EDGE - HALO:EDGE] = halo_l[every].astype(F32)
+
+        @pl.when(me < last)
+        def _():
+            to_prev(group).wait_recv()
+            near[every, EDGE + rows:EDGE + rows + HALO] = halo_r[every].astype(F32)
 
     def gated_layer(layer, m):
         w = win.at[layer]
@@ -142,8 +154,6 @@
                 f = f + jnp.dot(op, w[tap, :, col:col + COLS], preferred_element_type=F32)
                 g = g + jnp.dot(op, w[tap, :, n_chan + col:n_chan + col + COLS], preferred_element_type=F32)
             gate[:m, col:col + COLS] = (jnp.tanh(f) * (0.5 * jnp.tanh(0.5 * g) + 0.5)).astype(BF16)
-
-    start_weights(n_near - 1)
 
     def near_phase(group):
         seqs = range(group * in_group, (group + 1) * in_group)
@@ -172,8 +182,8 @@
             for col in range(0, n_chan, COLS):
                 res = jnp.dot(gate[:m], wres[layer, :, col:col + COLS], preferred_element_type=F32).reshape(in_group, size, COLS)
                 near[every, lo:hi, col:col + COLS] = near[every, lo:hi, col:col + COLS] + res
-            if group == 0 and layer + 1 < n_rows:
-                heard_column(layer + 1)
+            if group == 0 and layer + 2 < n_rows:
+                heard_column(layer + 2)
             if layer < n_near - 1:
                 @pl.when(me == 0)
                 def _():
@@ -194,26 +204,21 @@
                                             recv_sem=mid_recv.at[group], device_id={'sp': dst}, device_id_type=MESH)
 
     def send_mid(group):
-        @pl.loop(1, n_dev)
+        @pl.loop(1, n_dev, unroll=UNROLL)
         def _(k):
             mid_copy(group, lax.rem(me + k, n_dev)).start()
 
         mid_in[group, me] = mid_out[group, me]
 
     for group in range(GROUPS):
+        take_halo(group)
+        if group == 0:
+            start_weights(n_near - 1)
         near_phase(group)
         if group == 0:
-            for step in range(n_near + 1, n_rows):
+            for step in range(n_near + 2, n_rows):
                 heard_column(step)
         send_mid(group)
-
-    for col in range(0, n_skip, COLS):
-        skip = jnp.zeros((n_seq * rows, COLS), F32)
-        for layer in range(n_near):
-            skip = skip + jnp.dot(near_gate[:, layer * n_chan:(layer + 1) * n_chan], wskip[layer, :, col:col + COLS], preferred_element_type=F32)
-        near_skip[:, :, col:col + COLS] = skip.reshape(n_seq, rows, COLS)
-    skip_copy = pltpu.make_async_copy(near_skip, skip_out, own_sem.at[GROUPS])
-    skip_copy.start()
 
     def end_copy(group, dst):
         return pltpu.make_async_remote_copy(src_ref=end_out.at[group, dst // 2, lax.rem(dst, 2)], dst_ref=home.at[group, me],
@@ -223,13 +228,18 @@
         return pltpu.make_async_copy(end_out.at[group, me // 2, lax.rem(me, 2)], home.at[group, me], own_sem.at[group])
 
     def send_home(group):
-        @pl.loop(0, n_dev)
-        def _(k):
-            dst = k + 1 - 2 * lax.rem(k, 2)
-
-            @pl.when(dst != me)
-            def _():
-                end_copy(group, dst).start()
+        if group == 0:
+            @pl.loop(1, n_dev, unroll=UNROLL)
+            def _(k):
+                end_copy(group, lax.rem(me + k, n_dev)).start()
+
+        else:
+            skipped = me + 1 - 2 * lax.rem(me, 2)
+
+            @pl.loop(0, n_dev - 1, unroll=UNROLL)
+            def _(k):
+                place = k + jnp.where(k >= skipped, 1, 0)
+                end_copy(group, place + 1 - 2 * lax.rem(place, 2)).start()
 
         own_copy(group).start()
 
@@ -237,6 +247,10 @@
 
     def wait_all(ref, sem):
         pltpu.make_async_copy(ref.at[others], ref.at[others], sem).wait()
+
+    for layer in range(n_near, n_layers):
+        for copy in weight_copies(layer):
+            copy.wait()
 
     for group in range(GROUPS):
         wait_all(mid_in.at[group], mid_recv.at[group])
@@ -248,9 +262,6 @@
             for tap in range(3):
                 off = pad + (tap - 1) * dist
                 lhs[:far_rows, tap * n_chan:(tap + 1) * n_chan] = far[group, off:off + far_rows].astype(BF16)
-            if group == 0:
-                for copy in weight_copies(layer):
-                    copy.wait()
             gated_layer(layer, far_rows)
             for col in range(0, n_chan, COLS):
                 res = jnp.dot(gate[:far_rows], wres[layer, :, col:col + COLS], preferred_element_type=F32)
@@ -266,6 +277,14 @@
                 end_out[group, :, at, which * TILE:(which + 1) * TILE] = block
         send_home(group)
 
+    for col in range(0, n_skip, COLS):
+        skip = jnp.zeros((n_seq * rows, COLS), F32)
+        for layer in range(n_near):
+            skip = skip + jnp.dot(near_gate[:, layer * n_chan:(layer + 1) * n_chan], wskip[layer, :, col:col + COLS], preferred_element_type=F32)
+        near_skip[:, :, col:col + COLS] = skip.reshape(n_seq, rows, COLS)
+    skip_copy = pltpu.make_async_copy(near_skip, skip_out, own_sem.at[GROUPS])
+    skip_copy.start()
+
     for group in range(GROUPS):
         wait_all(mid_out.at[group], mid_send.at[group])
     for group in range(GROUPS):
@@ -275,13 +294,14 @@
         own_copy(group).wait()
     skip_copy.wait()
 
-    @pl.when(me < last)
-    def _():
-        to_next().wait_send()
-
-    @pl.when(me > 0)
-    def _():
-        to_prev().wait_send()
+    for group in range(GROUPS):
+        @pl.when(me < last)
+        def _():
+            to_next(group).wait_send()
+
+        @pl.when(me > 0)
+        def _():
+            to_prev(group).wait_send()
 
 
 def assemble_kernel(home, skip, h_out, s_out, h_rows, s_rows, sems):
@@ -343,7 +363,7 @@
                 pltpu.VMEM((GROUPS, far_rows + 2 * pad, n_chan), F32), pltpu.VMEM((GROUPS, far_rows, n_skip), F32),
                 pltpu.VMEM((GROUPS, n_dev // 2, 2, 2 * TILE, lanes), F32),
                 pltpu.VMEM((m_max, 3 * n_chan), BF16), pltpu.VMEM((m_max, n_chan), BF16), pltpu.VMEM((n_seq * rows, n_near * n_chan), BF16),
-                dma((GROUPS + 1,)), dma((n_layers, 3)), dma((2,)), dma((2,)), pltpu.SemaphoreType.REGULAR((max(n_dev // ROW - 1, 1),)), *[dma((GROUPS,)) for _ in range(4)],
+                dma((GROUPS + 1,)), dma((n_layers, 3)), dma((2, GROUPS)), dma((2, GROUPS)), pltpu.SemaphoreType.REGULAR((max(n_dev // ROW - 1, 1),)), *[dma((GROUPS,)) for _ in range(4)],
             ],
             compiler_params=pltpu.CompilerParams(collective_id=0, has_side_effects=True, vmem_limit_bytes=52 * 2 ** 20),
             name='dilated_stack',

time: 43 us -> 41.6 us (0.967)
  Pallas kernels: 41.1 us -> 39.3 us
    pallas_call x1, Pallas kernels: 40.1 us -> 38.3 us  [local_stack(): pl.pallas_call(functools.partial(stack_kernel, n_dev, n_near), out_shape=...]
where the time goes in v6:
time: 41.6 us; the launch traced here: 41.1 us
  Pallas kernels  39.3 us (94%)
  local copies, waits for them, and re-layouts  0.94 us (2%)
  between operations  0.81 us (2%)
    pallas_call x1, Pallas kernels, local_stack(): pl.pallas_call(functools.partial(stack_kernel, n_dev, n_near), out_shape=...  38.3 us
    pallas_call x1, Pallas kernels, local_stack(): pl.pallas_call(assemble_kernel, out_shape=(jax.ShapeDtypeStruct((n_seq, r...  1.05 us
    unnamed x2, local copies, waits for them, and re-layouts  0.94 us

profile of v6, /device:TPU:97, one launch (start us, length us, event | category | flops | bytes accessed | tf_op | source)
XLA Modules:
  0.0 41.1 jit_solution(13484135549532465212)
XLA Ops:
  0.6 0.0 copy-start
  0.6 0.9 %copy-done = bf16[4,64,512]{2,1,0:T(8,128)(2,1)S(1)} copy-done((bf16[4,64,512]{2,1,0:T(8,128)(2,1)S(1)}, bf16[4,64,512]{2,1,0:T(8,128)(2,1)}, u32[]{:S(2)}) %copy-start) | copy-done | bytes 262168
  1.6 38.3 %dilated_stack.1 = (f32[2,32,16,256]{3,2,1,0:T(8,128)S(1)}, f32[4,64,512]{2,1,0:T(8,128)S(1)}) custom-call(bf16[4,64,512]{2,1,0:T(8,128)(2,1)S(1)} %copy-done, bf16[11,3,512,1024]{3,2,1,0:T(8,128)(2,1)} %win_hbm.1, bf16[11,512,512]{2,1,0:T(8,128)(2,1)} %wres_hbm.1, bf16[11,512,512]{2,1,0:T(8,128)(2,1)} %wskip_hbm.1), custom_call_target="tpu_custom_call" | custom-call | tf_op jit(solution)/shard_map/dilated_stack/pallas_call | solution.py:353
  39.9 1.1 %assemble.1 = (f32[4,64,512]{2,1,0:T(8,128)}, f32[4,64,512]{2,1,0:T(8,128)}) custom-call(f32[2,32,16,256]{3,2,1,0:T(8,128)S(1)} %get-tuple-element.4.home, f32[4,64,512]{2,1,0:T(8,128)S(1)} %get-tuple-element.5.skip), custom_call_target="tpu_custom_call" | custom-call | tf_op jit(solution)/shard_map/assemble/pallas_call | solution.py:371
Async XLA Ops:
  0.6 1.0 %copy-start = (bf16[4,64,512]{2,1,0:T(8,128)(2,1)S(1)}, bf16[4,64,512]{2,1,0:T(8,128)(2,1)}, u32[]{:S(2)}) copy-start(bf16[4,64,512]{2,1,0:T(8,128)(2,1)} %xv.1) | copy-start | bytes 786436

commit v7 on v6

--- a/solution.py
+++ b/solution.py
@@ -206,7 +206,7 @@
     def send_mid(group):
         @pl.loop(1, n_dev, unroll=UNROLL)
         def _(k):
-            mid_copy(group, lax.rem(me + k, n_dev)).start()
+            mid_copy(group, lax.rem(me + n_dev - k, n_dev)).start()
 
         mid_in[group, me] = mid_out[group, me]
 

time: 41.6 us -> 41.4 us (level)
  no operation moved by 1% of the time
where the time goes in v7:
time: 41.4 us; the launch traced here: 40.9 us
  Pallas kernels  39.2 us (95%)
  local copies, waits for them, and re-layouts  0.94 us (2%)
  between operations  0.81 us (2%)
    pallas_call x1, Pallas kernels, local_stack(): pl.pallas_call(functools.partial(stack_kernel, n_dev, n_near), out_shape=...  38.1 us
    pallas_call x1, Pallas kernels, local_stack(): pl.pallas_call(assemble_kernel, out_shape=(jax.ShapeDtypeStruct((n_seq, r...  1.05 us
    unnamed x2, local copies, waits for them, and re-layouts  0.94 us

profile of v7, /device:TPU:97, one launch (start us, length us, event | category | flops | bytes accessed | tf_op | source)
XLA Modules:
  0.0 40.9 jit_solution(1462730582693977724)
XLA Ops:
  0.6 0.0 copy-start
  0.6 0.9 %copy-done = bf16[4,64,512]{2,1,0:T(8,128)(2,1)S(1)} copy-done((bf16[4,64,512]{2,1,0:T(8,128)(2,1)S(1)}, bf16[4,64,512]{2,1,0:T(8,128)(2,1)}, u32[]{:S(2)}) %copy-start) | copy-done | bytes 262168
  1.6 38.1 %dilated_stack.1 = (f32[2,32,16,256]{3,2,1,0:T(8,128)S(1)}, f32[4,64,512]{2,1,0:T(8,128)S(1)}) custom-call(bf16[4,64,512]{2,1,0:T(8,128)(2,1)S(1)} %copy-done, bf16[11,3,512,1024]{3,2,1,0:T(8,128)(2,1)} %win_hbm.1, bf16[11,512,512]{2,1,0:T(8,128)(2,1)} %wres_hbm.1, bf16[11,512,512]{2,1,0:T(8,128)(2,1)} %wskip_hbm.1), custom_call_target="tpu_custom_call" | custom-call | tf_op jit(solution)/shard_map/dilated_stack/pallas_call | solution.py:353
  39.7 1.1 %assemble.1 = (f32[4,64,512]{2,1,0:T(8,128)}, f32[4,64,512]{2,1,0:T(8,128)}) custom-call(f32[2,32,16,256]{3,2,1,0:T(8,128)S(1)} %get-tuple-element.4.home, f32[4,64,512]{2,1,0:T(8,128)S(1)} %get-tuple-element.5.skip), custom_call_target="tpu_custom_call" | custom-call | tf_op jit(solution)/shard_map/assemble/pallas_call | solution.py:371
Async XLA Ops:
  0.6 1.0 %copy-start = (bf16[4,64,512]{2,1,0:T(8,128)(2,1)S(1)}, bf16[4,64,512]{2,1,0:T(8,128)(2,1)}, u32[]{:S(2)}) copy-start(bf16[4,64,512]{2,1,0:T(8,128)(2,1)} %xv.1) | copy-start | bytes 786436
